TPU v7x, 128 devices: a whole 4x4x4 slice. The times are simulated.
128 devices in a mesh: dp: 16 (over x, y), mp: 8 (over z, core).
Axes of the slice: x: 4, y: 4, z: 4, core: 2. Of those that a mesh axis runs over, the one named last changes fastest.
Arguments:
- patches: bfloat16 [768, 64, 1024], P(('dp', 'mp')), may hold values from -6 to 6
- gain_first: float32 [1024], replicated, may hold values from 0.1 to 1.9
- joint_weight: bfloat16 [1024, 3, 1024], P('dp', None, 'mp'), may hold values from -0.1875 to 0.1875
- head_scale: float32 [16], P('mp'), may hold values from 2 to 32
- output_weight: bfloat16 [1024, 1024], P('mp', 'dp'), may hold values from -0.1875 to 0.1875
- gain_second: float32 [1024], replicated, may hold values from 0.3 to 3
- up_weight: bfloat16 [1024, 4096], P('dp', 'mp'), may hold values from -0.1875 to 0.1875
- down_weight: bfloat16 [4096, 1024], P('mp', 'dp'), may hold values from -0.09375 to 0.09375
- gain_final: float32 [1024], replicated, may hold values from 0.1 to 1.9
- project_weight: bfloat16 [1024, 768], replicated, may hold values from -0.1875 to 0.1875
- text_bank: bfloat16 [12288, 768], P(('dp', 'mp')), may hold values from -20000 to 20000
- captions: int32 [768], replicated, may hold values from 0 to 12287
- reference_loss: float32 [768], P(('dp', 'mp')), may hold values from 2 to 20
Outputs:
- learnability: float32 [768], P(('dp', 'mp'))
All inputs are finite; a program needn't handle non-finite values.
Results may differ from a plain program's by a relative error of at most 0.018.
Values may be sent and summed in bfloat16 or wider, within the bound.
No kernel may reach another device: no remote copies, remote signals or barrier semaphores. Data moves between devices by JAX's collectives and lax.ppermute only.
A program may use at most 128 MiB of HBM per device.

v0:
```python
import jax
import jax.numpy as jnp
from jax import lax
from jax.experimental import pallas as pl
from jax.experimental.pallas import tpu as pltpu
from jax.sharding import PartitionSpec as P


AXES = ("dp", "mp")
DEVICES = [(x, y, z, c) for x in range(4) for y in range(4) for z in range(4) for c in range(2)]
F32 = jnp.float32
BF16 = jnp.bfloat16
NT = (((1,), (1,)), ((), ()))


def device_id(x, y, z, c):
    return x * 32 + y * 8 + z * 2 + c


def shift_pairs(axis, step):
    pairs = []
    for place in DEVICES:
        goal = list(place)
        goal[axis] = (goal[axis] + (step if place[3] == 0 else -step)) % 4
        pairs.append((device_id(*place), device_id(*goal)))
    return pairs


SWAP = [(i, i ^ 1) for i in range(128)]


def swapped(array):
    return lax.ppermute(array, AXES, SWAP)


def ring(array, axis):
    ahead = lax.ppermute(array, AXES, shift_pairs(axis, 1))
    behind = lax.ppermute(array, AXES, shift_pairs(axis, -1))
    far = lax.ppermute(ahead, AXES, shift_pairs(axis, 1))
    return [array, ahead, behind, far]


def call(body, outs, args, grid=(1,), ins=None, out_specs=None, scratch=(), prefetch=0, limit=16):
    whole = lambda s: pl.BlockSpec(s, lambda *_: (0,) * len(s))
    ins = ins or [None] * (len(args) - prefetch)
    ins = [b or whole(a.shape) for b, a in zip(ins, args[prefetch:])]
    out_specs = out_specs or [whole(o.shape) for o in outs]
    return pl.pallas_call(
        body,
        out_shape=outs,
        grid_spec=pltpu.PrefetchScalarGridSpec(
            num_scalar_prefetch=prefetch, grid=grid, in_specs=ins, out_specs=out_specs, scratch_shapes=list(scratch)
        ),
        compiler_params=pltpu.CompilerParams(vmem_limit_bytes=limit << 20),
    )(*args)


def norm_rows(values, gain):
    centre = values - jnp.mean(values, axis=-1, keepdims=True)
    spread = jnp.mean(centre * centre, axis=-1, keepdims=True)
    return centre * lax.rsqrt(spread + 1e-06) * gain


def split(values):
    high = values.astype(BF16)
    return high, (values - high.astype(F32)).astype(BF16)


def block_ones(size, block):
    row = lax.broadcasted_iota(jnp.int32, (size, size), 0) // block
    col = lax.broadcasted_iota(jnp.int32, (size, size), 1) // block
    return (row == col).astype(F32).astype(BF16)


def norm_kernel(own, other, gain, own_out, other_out):
    own_out[...] = norm_rows(own[...].astype(F32), gain[...]).astype(BF16)
    other_out[...] = norm_rows(other[...].astype(F32), gain[...]).astype(BF16)


def pack_kernel(up, down, text, scale, out):
    out[0:64] = up[...]
    out[64:128] = down[...]
    out[128:224] = text[:, 0:512]
    out[224:272, 0:256] = text[0:48, 512:768]
    out[224:272, 256:512] = text[48:96, 512:768]
    out[272:288] = scale[...]


def unpack_kernel(m0, m1, m2, m3, ups, downs, texts, scales):
    for r, m in enumerate((m0, m1, m2, m3)):
        ups[r * 64 : (r + 1) * 64] = m[0:64]
        downs[r * 64 : (r + 1) * 64] = m[64:128]
        texts[r * 96 : (r + 1) * 96, 0:512] = m[128:224]
        texts[r * 96 : r * 96 + 48, 512:768] = m[224:272, 0:256]
        texts[r * 96 + 48 : (r + 1) * 96, 512:768] = m[224:272, 256:512]
        scales[r * 8 : (r + 1) * 8] = jnp.broadcast_to(
            jnp.sum(m[272:288, 0:128].astype(F32), axis=0, keepdims=True), (8, 128)
        )


def join_kernel(a, b, c, d, out):
    for r, part in enumerate((a, b, c, d)):
        out[r * 256 : (r + 1) * 256] = part[...]


def interleave_kernel(a, b, c, d, out):
    for r, part in enumerate((a, b, c, d)):
        for k in range(4):
            out[(k * 4 + r) * 64 : (k * 4 + r + 1) * 64] = part[k * 64 : (k + 1) * 64]


def attend_kernel(own, other, piece, scales, out):
    scale = scales[0:1]
    ones = block_ones(256, 64)
    lane = lax.broadcasted_iota(jnp.int32, (64, 128), 1)
    first = lane < 64
    nil = jnp.zeros((64, 128), F32)
    for side, rows in enumerate((own, other)):
        joint = jnp.dot(rows[...], piece[:, 0:384], preferred_element_type=F32)
        pair = joint[:, 0:256]
        high, low = split(pair * pair)
        squares = jnp.dot(high, ones, preferred_element_type=F32) + jnp.dot(low, ones, preferred_element_type=F32)
        unit = pair * lax.rsqrt(squares + 1e-06)
        for i in range(6):
            at = slice(i * 64, (i + 1) * 64)
            query = unit[at, 0:128].astype(BF16)
            key = unit[at, 128:256]
            value = joint[at, 256:384]
            keys = jnp.concatenate([jnp.where(first, key, nil), jnp.where(first, nil, key)], axis=0).astype(BF16)
            values = jnp.concatenate([jnp.where(first, value, nil), jnp.where(first, nil, value)], axis=0).astype(BF16)
            scores = lax.dot_general(query, keys, NT, preferred_element_type=F32)
            weights = jnp.exp(scores * scale).astype(BF16)
            mixed = jnp.dot(weights, values, preferred_element_type=F32)
            total = jnp.dot(weights, ones[0:128, 0:128], preferred_element_type=F32)
            out[side * 384 + i * 64 : side * 384 + (i + 1) * 64, :] = (mixed / total).astype(BF16)


def output_kernel(h0, h1, h2, h3, p0, p1, p2, p3, own, other):
    heads = jnp.concatenate([h0[...], h1[...], h2[...], h3[...]], axis=1)
    weight = jnp.concatenate([p0[...], p1[...], p2[...], p3[...]], axis=1)
    own[...] = lax.dot_general(heads[0:384], weight, NT, preferred_element_type=F32)
    other[...] = lax.dot_general(heads[384:768], weight, NT, preferred_element_type=F32).astype(BF16)


def residual_kernel(patches, own, other, gain, normed, pooled):
    residual = patches[...].astype(F32) + own[...] + other[...].astype(F32)
    normed[...] = norm_rows(residual, gain[...]).astype(BF16)
    pooled[0:6] = jnp.sum(residual.reshape(6, 64, 1024), axis=1) * (1.0 / 64)
    pooled[6:8] = jnp.zeros((2, 1024), F32)


def up_kernel(place, own, other, p0, p1, p2, p3, mean, weight):
    for r, piece in enumerate((p0, p1, p2, p3)):
        for j in range(4):
            at = pl.multiple_of(place[r * 4 + j] * 64, 64)
            weight[pl.ds(at, 64), :] = piece[j * 64 : (j + 1) * 64, :]
    for side, rows in enumerate((own, other)):
        upper = jnp.dot(rows[...], weight[...], preferred_element_type=F32)
        hidden = (0.5 * upper * (1.0 + lax.erf(upper * 0.7071067811865476))).astype(BF16).astype(F32)
        mean[side * 8 : side * 8 + 6, :] = jnp.sum(hidden.reshape(6, 64, 512), axis=1) * (1.0 / 64)
        mean[side * 8 + 6 : side * 8 + 8, :] = jnp.zeros((2, 512), F32)


def down_kernel(place, mean, p0, p1, p2, p3, own, other, weight):
    for r, piece in enumerate((p0, p1, p2, p3)):
        for j in range(4):
            at = pl.multiple_of(place[r * 4 + j] * 64, 64)
            for k in range(4):
                weight[pl.ds(at, 64), k * 512 : (k + 1) * 512] = piece[(j * 4 + k) * 64 : (j * 4 + k + 1) * 64, :]
    high, low = split(mean[...])
    both = jnp.concatenate([high, low], axis=0)
    product = lax.dot_general(both, weight[...], NT, preferred_element_type=F32)
    product = product[0:16] + product[16:32]
    own[...] = product[0:8]
    other[...] = product[8:16]


def final_kernel(pooled, own, other, gain, project, units):
    total = pooled[...] + own[...] + other[...]
    normed = norm_rows(total, gain[...]).astype(BF16)
    embedded = jnp.dot(normed, project[...], preferred_element_type=F32)
    units[...] = (
        embedded * lax.rsqrt(jnp.sum(embedded * embedded, axis=-1, keepdims=True) + 1e-06)
    ).astype(BF16)


def logits_kernel(units, texts, wanted, ids, out):
    logits = lax.dot_general(units[...], texts[...], NT, preferred_element_type=F32)
    highest = jnp.max(logits, axis=1, keepdims=True)
    total = jnp.sum(jnp.exp(logits - highest), axis=1, keepdims=True)
    matched = jnp.sum(jnp.where(wanted[...] == ids[...], logits, 0.0), axis=1, keepdims=True)
    lane = lax.broadcasted_iota(jnp.int32, (128, 128), 1)
    out[...] = jnp.where(lane == 0, highest, jnp.where(lane == 1, total, matched))


def loss_kernel(parts, loss):
    highest = parts[0]
    for i in range(1, 16):
        highest = jnp.maximum(highest, parts[i])
    highest = highest[:, 0:1]
    total = jnp.zeros((8, 1), F32)
    matched = jnp.zeros((8, 1), F32)
    for i in range(16):
        part = parts[i]
        total = total + part[:, 1:2] * jnp.exp(part[:, 0:1] - highest)
        matched = matched + part[:, 2:3]
    loss[...] = jnp.broadcast_to(highest + jnp.log(total) - matched, (8, 128))


def shards(
    patches,
    gain_first,
    joint_weight,
    head_scale,
    output_weight,
    gain_second,
    up_weight,
    down_weight,
    gain_final,
    project_weight,
    text_bank,
    captions,
    reference_loss,
):
    dp, mp = lax.axis_index("dp"), lax.axis_index("mp")
    ix, iy, iz, core = dp // 4, dp % 4, mp // 2, mp % 2
    sign = 1 - 2 * core
    offsets = jnp.stack([0 * sign, -sign, sign, 0 * sign + 2])
    rx, ry, rz = (ix + offsets + 4) % 4, (iy + offsets + 4) % 4, (iz + offsets + 4) % 4
    by_y_x = (rx[None, :] * 4 + ry[:, None]).reshape(16).astype(jnp.int32)
    by_x_y = (rx[:, None] * 4 + ry[None, :]).reshape(16).astype(jnp.int32)

    rows = patches.reshape(384, 1024)
    rows_other = swapped(rows)
    sds = jax.ShapeDtypeStruct

    lanes = jnp.repeat(head_scale, 64)
    high = lax.reduce_precision(lanes, 8, 7)
    middle = lax.reduce_precision(lanes - high, 8, 7)
    low = lanes - high - middle
    scale_rows = jnp.pad(jnp.stack([high, middle, low]), ((0, 13), (0, 384))).astype(BF16)
    message = call(pack_kernel, [sds((288, 512), BF16)], [up_weight, down_weight.T, text_bank, scale_rows])[0]
    messages = ring(message, 2)
    shard_a = jnp.concatenate([joint_weight.reshape(64, 384), output_weight.T], axis=1)
    plane_a = lax.all_to_all(jnp.broadcast_to(shard_a[None], (16, 64, 512)), "dp", 0, 0, tiled=True)
    pieces_a = ring(plane_a.reshape(1024, 512), 2)
    first_b, first_c, texts_own, scales = call(
        unpack_kernel,
        [sds((256, 512), BF16), sds((256, 512), BF16), sds((384, 768), BF16), sds((32, 128), F32)],
        messages,
    )
    second_b = call(interleave_kernel, [sds((1024, 512), BF16)], ring(first_b, 1))[0]
    second_c = call(join_kernel, [sds((1024, 512), BF16)], ring(first_c, 0))[0]
    pieces_b = ring(second_b, 0)
    pieces_c = ring(second_c, 1)
    texts = jnp.concatenate([texts_own, swapped(texts_own)], axis=0)

    gain_row = gain_first.reshape(1, 1024)
    normed_own, normed_other = call(norm_kernel, [sds((384, 1024), BF16)] * 2, [rows, rows_other, gain_row])
    heads = []
    for r, piece in enumerate(pieces_a):
        heads += call(
            attend_kernel,
            [sds((768, 128), BF16)],
            [normed_own, normed_other, piece, scales],
            ins=[None, None, None, pl.BlockSpec((8, 128), lambda *_, r=r: (r, 0))],
        )
    last = pl.BlockSpec((1024, 128), lambda *_: (0, 3))
    part_own, part_other = call(
        output_kernel, [sds((384, 1024), F32), sds((384, 1024), BF16)], [*heads, *pieces_a], ins=[None] * 4 + [last] * 4
    )
    normed_two, pooled = call(
        residual_kernel,
        [sds((384, 1024), BF16), sds((8, 1024), F32)],
        [rows, part_own, swapped(part_other), gain_second.reshape(1, 1024)],
    )
    quarter = pl.BlockSpec((256, 512), lambda i, *_: (i, 0))
    mean = call(
        up_kernel,
        [sds((16, 2048), F32)],
        [by_x_y, normed_two, swapped(normed_two), *pieces_b],
        grid=(4,),
        ins=[None] * 2 + [quarter] * 4,
        out_specs=[pl.BlockSpec((16, 512), lambda i, *_: (0, i))],
        scratch=[pltpu.VMEM((1024, 512), BF16)],
        prefetch=1,
    )[0]
    feed_own, feed_other = call(
        down_kernel,
        [sds((8, 1024), F32)] * 2,
        [by_y_x, mean, *pieces_c],
        scratch=[pltpu.VMEM((1024, 2048), BF16)],
        limit=24,
        prefetch=1,
    )
    units = call(
        final_kernel,
        [sds((8, 768), BF16)],
        [pooled, feed_own, swapped(feed_other), gain_final.reshape(1, 1024), project_weight],
    )[0]

    rz_other = (iz - offsets + 4) % 4
    holders = jnp.concatenate([rz * 2 + core, rz_other * 2 + (1 - core)])
    ids = ((dp * 8 + holders)[:, None] * 96 + jnp.arange(96)[None, :]).reshape(1, 768).astype(jnp.int32)
    wanted = lax.dynamic_slice_in_dim(captions.reshape(16, 8, 6), mp, 1, axis=1)[:, 0]
    wanted = jnp.pad(wanted, ((0, 0), (0, 2)), constant_values=-1).reshape(128, 1)

    everyone = lax.all_to_all(jnp.broadcast_to(units[None], (16, 8, 768)), "dp", 0, 0, tiled=True)
    parts = call(logits_kernel, [sds((128, 128), F32)], [everyone.reshape(128, 768), texts, wanted, ids])[0]
    parts = lax.all_to_all(parts.reshape(16, 8, 128), "dp", 0, 0, tiled=True)
    loss = call(loss_kernel, [sds((8, 128), F32)], [parts])[0]
    return loss[0:6, 0] - reference_loss


def solution(mesh):
    placed = (
        P(("dp", "mp"), None, None),
        P(),
        P("dp", None, "mp"),
        P("mp"),
        P("mp", "dp"),
        P(),
        P("dp", "mp"),
        P("mp", "dp"),
        P(),
        P(),
        P(("dp", "mp"), None),
        P(),
        P(("dp", "mp")),
    )

    return jax.shard_map(shards, mesh=mesh, in_specs=placed, out_specs=P(("dp", "mp")), check_vma=False)
```

profile of v0, /device:TPU:1, one launch (start us, length us, event | category | flops | bytes accessed | tf_op | source)
XLA Modules:
  0.0 163.1 jit_solution(1931273437519147166)
XLA Ops:
  0.0 0.8 copy-done
  0.8 0.7 pad_maximum_fusion.1
  1.6 1.1 broadcast_in_dim.6
  2.7 7.6 %all-to-all-start = ((bf16[16,64,512]{2,1,0:T(8,128)(2,1)}), bf16[16,64,512]{2,1,0:T(8,128)(2,1)S(1)}, u32[]{:S(2)}, u32[]{:S(2)}) async-start(bf16[16,64,512]{2,1,0:T(8,128)(2,1)} %broadcast_in_dim.6), calls=%async_computation | async-start | bytes 2097152 | tf_op jit(solution)/shard_map/all_to_all | solution.py:245
  10.4 15.5 %all-to-all-done = bf16[16,64,512]{2,1,0:T(8,128)(2,1)S(1)} async-done(((bf16[16,64,512]{2,1,0:T(8,128)(2,1)}), bf16[16,64,512]{2,1,0:T(8,128)(2,1)S(1)}, u32[]{:S(2)}, u32[]{:S(2)}) %all-to-all-start) | async-done | bytes 1048608 | tf_op jit(solution)/shard_map/all_to_all | solution.py:245
  25.9 3.8 %collective-permute-start.4 = (bf16[1024,512]{1,0:T(8,128)(2,1)S(1)}, bf16[1024,512]{1,0:T(8,128)(2,1)S(1)}, u32[]{:S(2)}, u32[]{:S(2)}) collective-permute-start(bf16[1024,512]{1,0:T(8,128)(2,1)S(1)} %bitcast.20), channel_id=1, source_target_pairs={{0,2},{1,7},{2,4},{3,1},{4,6},{5,3},{6,0},{7,5},{8,10},{9,15},{10,... | collective-permute-start | bytes 3145736 | tf_op jit(solution)/shard_map/ppermute | solution.py:37
  29.8 0.2 collective-permute-start.1
  30.0 1.3 collective-permute-start.2
  31.3 16.4 %collective-permute-done.1.m1 = bf16[288,512]{1,0:T(8,128)(2,1)S(1)} collective-permute-done((bf16[288,512]{1,0:T(8,128)(2,1)S(1)}, bf16[288,512]{1,0:T(8,128)(2,1)S(1)}, u32[]{:S(2)}, u32[]{:S(2)}) %collective-permute-start.1) | collective-permute-done | bytes 294944 | tf_op jit(solution)/shard_map/ppermute | solution.py:37
  47.8 3.1 %collective-permute-start.3 = (bf16[288,512]{1,0:T(8,128)(2,1)S(1)}, bf16[288,512]{1,0:T(8,128)(2,1)S(1)}, u32[]{:S(2)}, u32[]{:S(2)}) collective-permute-start(bf16[288,512]{1,0:T(8,128)(2,1)S(1)} %collective-permute-done.1.m1), channel_id=1, source_target_pairs={{0,2},{1,7},{2,4},{3,1},{4,6},{5,3},{6,0},{7,5},{8,10},{9,15},{10,... | collective-permute-start | bytes 884744 | tf_op jit(solution)/shard_map/ppermute | solution.py:39
  50.9 3.7 %collective-permute-done.3.m3 = bf16[288,512]{1,0:T(8,128)(2,1)S(1)} collective-permute-done((bf16[288,512]{1,0:T(8,128)(2,1)S(1)}, bf16[288,512]{1,0:T(8,128)(2,1)S(1)}, u32[]{:S(2)}, u32[]{:S(2)}) %collective-permute-start.3) | collective-permute-done | bytes 294944 | tf_op jit(solution)/shard_map/ppermute | solution.py:39
  54.6 0.8 copy-done.2
  55.4 1.2 collective-permute-start.9
  56.6 0.3 collective-permute-start.10
  56.9 3.1 %collective-permute-start.6 = (bf16[1024,512]{1,0:T(8,128)(2,1)S(1)}, bf16[1024,512]{1,0:T(8,128)(2,1)S(1)}, u32[]{:S(2)}, u32[]{:S(2)}) collective-permute-start(bf16[1024,512]{1,0:T(8,128)(2,1)S(1)} %collective-permute-done.4.piece.p1), channel_id=1, source_target_pairs={{0,2},{1,7},{2,4},{3,1},{4,6},{5,3},{6,0},{7,5},{8,10},{9,15},{10,... | collective-permute-start | bytes 3145736 | tf_op jit(solution)/shard_map/ppermute | solution.py:39
  60.0 1.1 collective-permute-start.15
  61.1 2.6 %collective-permute-start.11 = (bf16[256,512]{1,0:T(8,128)(2,1)S(1)}, bf16[256,512]{1,0:T(8,128)(2,1)S(1)}, u32[]{:S(2)}, u32[]{:S(2)}) collective-permute-start(bf16[256,512]{1,0:T(8,128)(2,1)S(1)} %collective-permute-done.9.b), channel_id=1, source_target_pairs={{0,8},{1,25},{2,10},{3,27},{4,12},{5,29},{6,14},{7,31},{8,16},{9,1... | collective-permute-start | bytes 786440 | tf_op jit(solution)/shard_map/ppermute | solution.py:39
  63.7 6.5 %collective-permute-start = (bf16[384,1024]{1,0:T(8,128)(2,1)}, bf16[384,1024]{1,0:T(8,128)(2,1)S(1)}, u32[]{:S(2)}, u32[]{:S(2)}) collective-permute-start(bf16[384,1024]{1,0:T(8,128)(2,1)} %bitcast.own.patches), channel_id=1, source_target_pairs={{0,1},{1,0},{2,3},{3,2},{4,5},{5,4},{6,7},{7,6},{8,9},{9,8},{10,11... | collective-permute-start | bytes 2359304 | tf_op jit(solution)/shard_map/ppermute | solution.py:33
  70.2 2.7 %collective-permute-start.17 = (bf16[256,512]{1,0:T(8,128)(2,1)S(1)}, bf16[256,512]{1,0:T(8,128)(2,1)S(1)}, u32[]{:S(2)}, u32[]{:S(2)}) collective-permute-start(bf16[256,512]{1,0:T(8,128)(2,1)S(1)} %collective-permute-done.15.b), channel_id=1, source_target_pairs={{0,32},{1,97},{2,34},{3,99},{4,36},{5,101},{6,38},{7,103},{8,40},{... | collective-permute-start | bytes 786440 | tf_op jit(solution)/shard_map/ppermute | solution.py:39
  72.9 4.0 %collective-permute-done.16.c = bf16[256,512]{1,0:T(8,128)(2,1)S(1)} collective-permute-done((bf16[256,512]{1,0:T(8,128)(2,1)S(1)}, bf16[256,512]{1,0:T(8,128)(2,1)S(1)}, u32[]{:S(2)}, u32[]{:S(2)}) %collective-permute-start.16) | collective-permute-done | bytes 262176 | tf_op jit(solution)/shard_map/ppermute | solution.py:38
  76.9 1.2 collective-permute-done.17.d
  78.2 3.7 %collective-permute-start.18 = (bf16[1024,512]{1,0:T(8,128)(2,1)S(1)}, bf16[1024,512]{1,0:T(8,128)(2,1)}, u32[]{:S(2)}, u32[]{:S(2)}) collective-permute-start(bf16[1024,512]{1,0:T(8,128)(2,1)S(1)} %shard_map.138.p0), channel_id=1, source_target_pairs={{0,8},{1,25},{2,10},{3,27},{4,12},{5,29},{6,14},{7,31},{8,16},{9,1... | collective-permute-start | bytes 3145736 | tf_op jit(solution)/shard_map/ppermute | solution.py:37
  81.9 2.1 %shard_map.127 = (bf16[384,1024]{1,0:T(8,128)(2,1)S(1)}, bf16[384,1024]{1,0:T(8,128)(2,1)S(1)}) custom-call(bf16[384,1024]{1,0:T(8,128)(2,1)} %bitcast.own.patches, bf16[384,1024]{1,0:T(8,128)(2,1)S(1)} %collective-permute-done.other, f32[1,1024]{1,0:T(1,128)S(1)} %bitcast.27), custom_call_target="tpu_custom_call" | custom-call | tf_op jit(solution)/shard_map/pallas_call | solution.py:48
  84.1 2.5 %shard_map.130.h0 = bf16[768,128]{1,0:T(8,128)(2,1)S(1)} custom-call(bf16[384,1024]{1,0:T(8,128)(2,1)S(1)} %get-tuple-element.17.own, bf16[384,1024]{1,0:T(8,128)(2,1)S(1)} %get-tuple-element.18.other, bf16[1024,512]{1,0:T(8,128)(2,1)S(1)} %bitcast.22, f32[32,128]{1,0:T(8,128)S(1)} %get-tuple-element.19.scales), custom_call_target="tpu_custom_call" | custom-call | tf_op jit(solution)/shard_map/pallas_call | solution.py:48
  86.6 2.5 %shard_map.131.h1 = bf16[768,128]{1,0:T(8,128)(2,1)S(1)} custom-call(bf16[384,1024]{1,0:T(8,128)(2,1)S(1)} %get-tuple-element.17.own, bf16[384,1024]{1,0:T(8,128)(2,1)S(1)} %get-tuple-element.18.other, bf16[1024,512]{1,0:T(8,128)(2,1)S(1)} %collective-permute-done.4.piece.p1, f32[32,128]{1,0:T(8,128)S(1)} %get-tuple-element.19.scales), custom_call_target="tpu_custom_call" | custom-call | tf_op jit(solution)/shard_map/pallas_call | solution.py:48
  89.2 2.5 %shard_map.132.h2 = bf16[768,128]{1,0:T(8,128)(2,1)S(1)} custom-call(bf16[384,1024]{1,0:T(8,128)(2,1)S(1)} %get-tuple-element.17.own, bf16[384,1024]{1,0:T(8,128)(2,1)S(1)} %get-tuple-element.18.other, bf16[1024,512]{1,0:T(8,128)(2,1)S(1)} %collective-permute-done.5.piece.p2, f32[32,128]{1,0:T(8,128)S(1)} %get-tuple-element.19.scales), custom_call_target="tpu_custom_call" | custom-call | tf_op jit(solution)/shard_map/pallas_call | solution.py:48
  91.7 2.5 %shard_map.133.h3 = bf16[768,128]{1,0:T(8,128)(2,1)S(1)} custom-call(bf16[384,1024]{1,0:T(8,128)(2,1)S(1)} %get-tuple-element.17.own, bf16[384,1024]{1,0:T(8,128)(2,1)S(1)} %get-tuple-element.18.other, bf16[1024,512]{1,0:T(8,128)(2,1)S(1)} %collective-permute-done.6.piece.p3, f32[32,128]{1,0:T(8,128)S(1)} %get-tuple-element.19.scales), custom_call_target="tpu_custom_call" | custom-call | tf_op jit(solution)/shard_map/pallas_call | solution.py:48
  94.2 1.1 shard_map.134
  95.3 1.9 %collective-permute-start.7 = (bf16[384,1024]{1,0:T(8,128)(2,1)S(1)}, bf16[384,1024]{1,0:T(8,128)(2,1)S(1)}, u32[]{:S(2)}, u32[]{:S(2)}) collective-permute-start(bf16[384,1024]{1,0:T(8,128)(2,1)S(1)} %get-tuple-element.21), channel_id=1, source_target_pairs={{0,1},{1,0},{2,3},{3,2},{4,5},{5,4},{6,7},{7,6},{8,9},{9,8},{10,11... | collective-permute-start | bytes 2359304 | tf_op jit(solution)/shard_map/ppermute | solution.py:33
  97.2 2.7 %collective-permute-start.14 = (bf16[1024,512]{1,0:T(8,128)(2,1)}, bf16[1024,512]{1,0:T(8,128)(2,1)}, u32[]{:S(2)}, u32[]{:S(2)}) collective-permute-start(bf16[1024,512]{1,0:T(8,128)(2,1)} %collective-permute-done.12.p1), channel_id=1, source_target_pairs={{0,32},{1,97},{2,34},{3,99},{4,36},{5,101},{6,38},{7,103},{8,40},{... | collective-permute-start | bytes 3145736 | tf_op jit(solution)/shard_map/ppermute | solution.py:39
  99.9 2.9 %collective-permute-start.20 = (bf16[1024,512]{1,0:T(8,128)(2,1)}, bf16[1024,512]{1,0:T(8,128)(2,1)}, u32[]{:S(2)}, u32[]{:S(2)}) collective-permute-start(bf16[1024,512]{1,0:T(8,128)(2,1)} %collective-permute-done.18.p1), channel_id=1, source_target_pairs={{0,8},{1,25},{2,10},{3,27},{4,12},{5,29},{6,14},{7,31},{8,16},{9,1... | collective-permute-start | bytes 3145736 | tf_op jit(solution)/shard_map/ppermute | solution.py:39
  102.8 2.7 %shard_map.135 = (bf16[384,1024]{1,0:T(8,128)(2,1)}, f32[8,1024]{1,0:T(8,128)S(1)}) custom-call(bf16[384,1024]{1,0:T(8,128)(2,1)} %bitcast.own.patches, f32[384,1024]{1,0:T(8,128)S(1)} %get-tuple-element.20.own, bf16[384,1024]{1,0:T(8,128)(2,1)S(1)} %collective-permute-done.7.other, f32[1,1024]{1,0:T(1,128)S(1)} %bitcast.28), custom_call_target="tpu_custom_call" | custom-call | tf_op jit(solution)/shard_map/pallas_call | solution.py:48
  105.7 15.8 %collective-permute-done.13.p2 = bf16[1024,512]{1,0:T(8,128)(2,1)} collective-permute-done((bf16[1024,512]{1,0:T(8,128)(2,1)S(1)}, bf16[1024,512]{1,0:T(8,128)(2,1)}, u32[]{:S(2)}, u32[]{:S(2)}) %collective-permute-start.13) | collective-permute-done | bytes 1048608 | tf_op jit(solution)/shard_map/ppermute | solution.py:38
  121.5 1.7 %collective-permute-start.22 = (bf16[384,768]{1,0:T(8,128)(2,1)}, bf16[384,768]{1,0:T(8,128)(2,1)}, u32[]{:S(2)}, u32[]{:S(2)}) collective-permute-start(bf16[384,768]{1,0:T(8,128)(2,1)} %copy-done.2), channel_id=1, source_target_pairs={{0,1},{1,0},{2,3},{3,2},{4,5},{5,4},{6,7},{7,6},{8,9},{9,8},{10,11... | collective-permute-start | bytes 1769480 | tf_op jit(solution)/shard_map/ppermute | solution.py:33
  123.4 7.7 %shard_map.137.mean = f32[16,2048]{1,0:T(8,128)S(1)} custom-call(s32[16]{0:T(128)S(1)} %add.222.place, bf16[384,1024]{1,0:T(8,128)(2,1)} %get-tuple-element.23.own, bf16[384,1024]{1,0:T(8,128)(2,1)} %collective-permute-done.8.other, bf16[1024,512]{1,0:T(8,128)(2,1)S(1)} %shard_map.136.p0, bf16[1024,512]{1,0:T(8,128)(2,1)} %collective-permute-done.12.p1, ...), custom_call_target="tpu_custom_call" | custom-call | tf_op jit(solution)/shard_map/pallas_call | solution.py:48
  131.2 3.6 %shard_map.139 = (f32[8,1024]{1,0:T(8,128)S(1)}, f32[8,1024]{1,0:T(8,128)S(1)}) custom-call(s32[16]{0:T(128)S(1)} %add.218.place, f32[16,2048]{1,0:T(8,128)S(1)} %shard_map.137.mean, bf16[1024,512]{1,0:T(8,128)(2,1)S(1)} %shard_map.138.p0, bf16[1024,512]{1,0:T(8,128)(2,1)} %collective-permute-done.18.p1, bf16[1024,512]{1,0:T(8,128)(2,1)S(1)} %collective-permute-done.19.p2, ...), custom_call_target="tpu_custom_call" | custom-call | tf_op jit(solution)/shard_map/pallas_call | solution.py:48
  134.8 0.7 collective-permute-start.21
  135.7 0.7 collective-permute-done.21.other
  136.4 1.4 copy-done.1
  137.8 0.5 shard_map.140
  138.3 0.7 broadcast_in_dim.8
  139.1 5.3 %all-to-all-start.1 = ((bf16[16,8,768]{2,1,0:T(8,128)(2,1)}), bf16[16,8,768]{2,1,0:T(8,128)(2,1)S(1)}, u32[]{:S(2)}, u32[]{:S(2)}) async-start(bf16[16,8,768]{2,1,0:T(8,128)(2,1)} %broadcast_in_dim.8), calls=%async_computation.1 | async-start | bytes 393216 | tf_op jit(solution)/shard_map/all_to_all | solution.py:308
  144.6 1.3 pad_maximum_fusion.texts
  145.9 5.5 %all-to-all-done.1 = bf16[16,8,768]{2,1,0:T(8,128)(2,1)S(1)} async-done(((bf16[16,8,768]{2,1,0:T(8,128)(2,1)}), bf16[16,8,768]{2,1,0:T(8,128)(2,1)S(1)}, u32[]{:S(2)}, u32[]{:S(2)}) %all-to-all-start.1) | async-done | bytes 196640 | tf_op jit(solution)/shard_map/all_to_all | solution.py:308
  151.4 0.7 shard_map.141
  152.1 10.1 %all_to_all.15.parts = f32[16,8,128]{2,1,0:T(8,128)S(1)} all-to-all(f32[16,8,128]{2,1,0:T(8,128)S(1)} %bitcast.25), channel_id=1, replica_groups=mesh['dp'=16,'mp'=8] {'dp'}, dimensions={0} | all-to-all | bytes 131072 | tf_op jit(solution)/shard_map/all_to_all | solution.py:310
  162.2 0.2 shard_map.142
  162.6 0.5 sub.54
  (66 shorter events, 1.5 us)
Async XLA Ops:
  0.0 0.8 copy-start
  1.5 8.7 %copy-start.10 = (f32[2]{0:T(128)S(1)}, f32[2]{0:T(128)}, u32[]{:S(2)}) copy-start(f32[2]{0:T(128)} %param.16) | copy-start | bytes 28
  1.5 28.2 %copy-start.3 = (bf16[96,768]{1,0:T(8,128)(2,1)S(1)}, bf16[96,768]{1,0:T(8,128)(2,1)}, u32[]{:S(2)}) copy-start(bf16[96,768]{1,0:T(8,128)(2,1)} %text.1) | copy-start | bytes 442372
  1.6 28.2 %copy-start.4 = (bf16[64,512]{1,0:T(8,128)(2,1)S(1)}, bf16[64,512]{1,0:T(8,128)(2,1)}, u32[]{:S(2)}) copy-start(bf16[64,512]{1,0:T(8,128)(2,1)} %up.1) | copy-start | bytes 196612
  1.6 28.2 %copy-start.5 = (bf16[512,64]{0,1:T(8,128)(2,1)S(1)}, bf16[512,64]{0,1:T(8,128)(2,1)}, u32[]{:S(2)}) copy-start(bf16[512,64]{0,1:T(8,128)(2,1)} %param.20) | copy-start | bytes 196612
  2.7 23.2 %all-to-all-start = ((bf16[16,64,512]{2,1,0:T(8,128)(2,1)}), bf16[16,64,512]{2,1,0:T(8,128)(2,1)S(1)}, u32[]{:S(2)}, u32[]{:S(2)}) async-start(bf16[16,64,512]{2,1,0:T(8,128)(2,1)} %broadcast_in_dim.6), calls=%async_computation | async-start | bytes 2097152 | tf_op jit(solution)/shard_map/all_to_all | solution.py:245
  25.9 31.0 %collective-permute-start.4 = (bf16[1024,512]{1,0:T(8,128)(2,1)S(1)}, bf16[1024,512]{1,0:T(8,128)(2,1)S(1)}, u32[]{:S(2)}, u32[]{:S(2)}) collective-permute-start(bf16[1024,512]{1,0:T(8,128)(2,1)S(1)} %bitcast.20), channel_id=1, source_target_pairs={{0,2},{1,7},{2,4},{3,1},{4,6},{5,3},{6,0},{7,5},{8,10},{9,15},{10,... | collective-permute-start | bytes 3145736 | tf_op jit(solution)/shard_map/ppermute | solution.py:37
  29.8 18.0 %collective-permute-start.1 = (bf16[288,512]{1,0:T(8,128)(2,1)S(1)}, bf16[288,512]{1,0:T(8,128)(2,1)S(1)}, u32[]{:S(2)}, u32[]{:S(2)}) collective-permute-start(bf16[288,512]{1,0:T(8,128)(2,1)S(1)} %shard_map.128.m0), channel_id=1, source_target_pairs={{0,2},{1,7},{2,4},{3,1},{4,6},{5,3},{6,0},{7,5},{8,10},{9,15},{10,... | collective-permute-start | bytes 884744 | tf_op jit(solution)/shard_map/ppermute | solution.py:37
  30.0 20.9 %collective-permute-start.2 = (bf16[288,512]{1,0:T(8,128)(2,1)S(1)}, bf16[288,512]{1,0:T(8,128)(2,1)S(1)}, u32[]{:S(2)}, u32[]{:S(2)}) collective-permute-start(bf16[288,512]{1,0:T(8,128)(2,1)S(1)} %shard_map.128.m0), channel_id=1, source_target_pairs={{0,6},{1,3},{2,0},{3,5},{4,2},{5,7},{6,4},{7,1},{8,14},{9,11},{10,... | collective-permute-start | bytes 884744 | tf_op jit(solution)/shard_map/ppermute | solution.py:38
  47.8 6.8 %collective-permute-start.3 = (bf16[288,512]{1,0:T(8,128)(2,1)S(1)}, bf16[288,512]{1,0:T(8,128)(2,1)S(1)}, u32[]{:S(2)}, u32[]{:S(2)}) collective-permute-start(bf16[288,512]{1,0:T(8,128)(2,1)S(1)} %collective-permute-done.1.m1), channel_id=1, source_target_pairs={{0,2},{1,7},{2,4},{3,1},{4,6},{5,3},{6,0},{7,5},{8,10},{9,15},{10,... | collective-permute-start | bytes 884744 | tf_op jit(solution)/shard_map/ppermute | solution.py:39
  54.6 0.8 copy-start.2
  55.4 5.7 %collective-permute-start.9 = (bf16[256,512]{1,0:T(8,128)(2,1)S(1)}, bf16[256,512]{1,0:T(8,128)(2,1)S(1)}, u32[]{:S(2)}, u32[]{:S(2)}) collective-permute-start(bf16[256,512]{1,0:T(8,128)(2,1)S(1)} %get-tuple-element.24.a), channel_id=1, source_target_pairs={{0,8},{1,25},{2,10},{3,27},{4,12},{5,29},{6,14},{7,31},{8,16},{9,1... | collective-permute-start | bytes 786440 | tf_op jit(solution)/shard_map/ppermute | solution.py:37
  56.6 7.0 %collective-permute-start.10 = (bf16[256,512]{1,0:T(8,128)(2,1)S(1)}, bf16[256,512]{1,0:T(8,128)(2,1)S(1)}, u32[]{:S(2)}, u32[]{:S(2)}) collective-permute-start(bf16[256,512]{1,0:T(8,128)(2,1)S(1)} %get-tuple-element.24.a), channel_id=1, source_target_pairs={{0,24},{1,9},{2,26},{3,11},{4,28},{5,13},{6,30},{7,15},{8,0},{9,17... | collective-permute-start | bytes 786440 | tf_op jit(solution)/shard_map/ppermute | solution.py:38
  56.9 32.2 %collective-permute-start.5 = (bf16[1024,512]{1,0:T(8,128)(2,1)S(1)}, bf16[1024,512]{1,0:T(8,128)(2,1)S(1)}, u32[]{:S(2)}, u32[]{:S(2)}) collective-permute-start(bf16[1024,512]{1,0:T(8,128)(2,1)S(1)} %bitcast.21), channel_id=1, source_target_pairs={{0,6},{1,3},{2,0},{3,5},{4,2},{5,7},{6,4},{7,1},{8,14},{9,11},{10,... | collective-permute-start | bytes 3145736 | tf_op jit(solution)/shard_map/ppermute | solution.py:38
  56.9 34.8 %collective-permute-start.6 = (bf16[1024,512]{1,0:T(8,128)(2,1)S(1)}, bf16[1024,512]{1,0:T(8,128)(2,1)S(1)}, u32[]{:S(2)}, u32[]{:S(2)}) collective-permute-start(bf16[1024,512]{1,0:T(8,128)(2,1)S(1)} %collective-permute-done.4.piece.p1), channel_id=1, source_target_pairs={{0,2},{1,7},{2,4},{3,1},{4,6},{5,3},{6,0},{7,5},{8,10},{9,15},{10,... | collective-permute-start | bytes 3145736 | tf_op jit(solution)/shard_map/ppermute | solution.py:39
  60.0 10.2 %collective-permute-start.15 = (bf16[256,512]{1,0:T(8,128)(2,1)S(1)}, bf16[256,512]{1,0:T(8,128)(2,1)S(1)}, u32[]{:S(2)}, u32[]{:S(2)}) collective-permute-start(bf16[256,512]{1,0:T(8,128)(2,1)S(1)} %get-tuple-element.25.a), channel_id=1, source_target_pairs={{0,32},{1,97},{2,34},{3,99},{4,36},{5,101},{6,38},{7,103},{8,40},{... | collective-permute-start | bytes 786440 | tf_op jit(solution)/shard_map/ppermute | solution.py:37
  61.1 9.1 %collective-permute-start.11 = (bf16[256,512]{1,0:T(8,128)(2,1)S(1)}, bf16[256,512]{1,0:T(8,128)(2,1)S(1)}, u32[]{:S(2)}, u32[]{:S(2)}) collective-permute-start(bf16[256,512]{1,0:T(8,128)(2,1)S(1)} %collective-permute-done.9.b), channel_id=1, source_target_pairs={{0,8},{1,25},{2,10},{3,27},{4,12},{5,29},{6,14},{7,31},{8,16},{9,1... | collective-permute-start | bytes 786440 | tf_op jit(solution)/shard_map/ppermute | solution.py:39
  63.7 18.3 %collective-permute-start = (bf16[384,1024]{1,0:T(8,128)(2,1)}, bf16[384,1024]{1,0:T(8,128)(2,1)S(1)}, u32[]{:S(2)}, u32[]{:S(2)}) collective-permute-start(bf16[384,1024]{1,0:T(8,128)(2,1)} %bitcast.own.patches), channel_id=1, source_target_pairs={{0,1},{1,0},{2,3},{3,2},{4,5},{5,4},{6,7},{7,6},{8,9},{9,8},{10,11... | collective-permute-start | bytes 2359304 | tf_op jit(solution)/shard_map/ppermute | solution.py:33
  70.2 6.7 %collective-permute-start.16 = (bf16[256,512]{1,0:T(8,128)(2,1)S(1)}, bf16[256,512]{1,0:T(8,128)(2,1)S(1)}, u32[]{:S(2)}, u32[]{:S(2)}) collective-permute-start(bf16[256,512]{1,0:T(8,128)(2,1)S(1)} %get-tuple-element.25.a), channel_id=1, source_target_pairs={{0,96},{1,33},{2,98},{3,35},{4,100},{5,37},{6,102},{7,39},{8,104},... | collective-permute-start | bytes 786440 | tf_op jit(solution)/shard_map/ppermute | solution.py:38
  70.2 8.0 %collective-permute-start.17 = (bf16[256,512]{1,0:T(8,128)(2,1)S(1)}, bf16[256,512]{1,0:T(8,128)(2,1)S(1)}, u32[]{:S(2)}, u32[]{:S(2)}) collective-permute-start(bf16[256,512]{1,0:T(8,128)(2,1)S(1)} %collective-permute-done.15.b), channel_id=1, source_target_pairs={{0,32},{1,97},{2,34},{3,99},{4,36},{5,101},{6,38},{7,103},{8,40},{... | collective-permute-start | bytes 786440 | tf_op jit(solution)/shard_map/ppermute | solution.py:39
  72.9 9.0 %copy-start.6 = (f32[1024]{0:T(1024)S(1)}, f32[1024]{0:T(1024)}, u32[]{:S(2)}) copy-start(f32[1024]{0:T(1024)} %param.14) | copy-start | bytes 12292
  76.9 20.3 %collective-permute-start.12 = (bf16[1024,512]{1,0:T(8,128)(2,1)S(1)}, bf16[1024,512]{1,0:T(8,128)(2,1)}, u32[]{:S(2)}, u32[]{:S(2)}) collective-permute-start(bf16[1024,512]{1,0:T(8,128)(2,1)S(1)} %shard_map.136.p0), channel_id=1, source_target_pairs={{0,32},{1,97},{2,34},{3,99},{4,36},{5,101},{6,38},{7,103},{8,40},{... | collective-permute-start | bytes 3145736 | tf_op jit(solution)/shard_map/ppermute | solution.py:37
  78.2 21.7 %collective-permute-start.18 = (bf16[1024,512]{1,0:T(8,128)(2,1)S(1)}, bf16[1024,512]{1,0:T(8,128)(2,1)}, u32[]{:S(2)}, u32[]{:S(2)}) collective-permute-start(bf16[1024,512]{1,0:T(8,128)(2,1)S(1)} %shard_map.138.p0), channel_id=1, source_target_pairs={{0,8},{1,25},{2,10},{3,27},{4,12},{5,29},{6,14},{7,31},{8,16},{9,1... | collective-permute-start | bytes 3145736 | tf_op jit(solution)/shard_map/ppermute | solution.py:37
  94.2 8.6 %copy-start.7 = (f32[1024]{0:T(1024)S(1)}, f32[1024]{0:T(1024)}, u32[]{:S(2)}) copy-start(f32[1024]{0:T(1024)} %param.18) | copy-start | bytes 12292
  95.3 7.5 %collective-permute-start.7 = (bf16[384,1024]{1,0:T(8,128)(2,1)S(1)}, bf16[384,1024]{1,0:T(8,128)(2,1)S(1)}, u32[]{:S(2)}, u32[]{:S(2)}) collective-permute-start(bf16[384,1024]{1,0:T(8,128)(2,1)S(1)} %get-tuple-element.21), channel_id=1, source_target_pairs={{0,1},{1,0},{2,3},{3,2},{4,5},{5,4},{6,7},{7,6},{8,9},{9,8},{10,11... | collective-permute-start | bytes 2359304 | tf_op jit(solution)/shard_map/ppermute | solution.py:33
  97.2 24.2 %collective-permute-start.13 = (bf16[1024,512]{1,0:T(8,128)(2,1)S(1)}, bf16[1024,512]{1,0:T(8,128)(2,1)}, u32[]{:S(2)}, u32[]{:S(2)}) collective-permute-start(bf16[1024,512]{1,0:T(8,128)(2,1)S(1)} %shard_map.136.p0), channel_id=1, source_target_pairs={{0,96},{1,33},{2,98},{3,35},{4,100},{5,37},{6,102},{7,39},{8,104},... | collective-permute-start | bytes 3145736 | tf_op jit(solution)/shard_map/ppermute | solution.py:38
  97.2 26.2 %collective-permute-start.14 = (bf16[1024,512]{1,0:T(8,128)(2,1)}, bf16[1024,512]{1,0:T(8,128)(2,1)}, u32[]{:S(2)}, u32[]{:S(2)}) collective-permute-start(bf16[1024,512]{1,0:T(8,128)(2,1)} %collective-permute-done.12.p1), channel_id=1, source_target_pairs={{0,32},{1,97},{2,34},{3,99},{4,36},{5,101},{6,38},{7,103},{8,40},{... | collective-permute-start | bytes 3145736 | tf_op jit(solution)/shard_map/ppermute | solution.py:39
  99.9 31.3 %collective-permute-start.19 = (bf16[1024,512]{1,0:T(8,128)(2,1)S(1)}, bf16[1024,512]{1,0:T(8,128)(2,1)S(1)}, u32[]{:S(2)}, u32[]{:S(2)}) collective-permute-start(bf16[1024,512]{1,0:T(8,128)(2,1)S(1)} %shard_map.138.p0), channel_id=1, source_target_pairs={{0,24},{1,9},{2,26},{3,11},{4,28},{5,13},{6,30},{7,15},{8,0},{9,17... | collective-permute-start | bytes 3145736 | tf_op jit(solution)/shard_map/ppermute | solution.py:38
  99.9 31.3 %collective-permute-start.20 = (bf16[1024,512]{1,0:T(8,128)(2,1)}, bf16[1024,512]{1,0:T(8,128)(2,1)}, u32[]{:S(2)}, u32[]{:S(2)}) collective-permute-start(bf16[1024,512]{1,0:T(8,128)(2,1)} %collective-permute-done.18.p1), channel_id=1, source_target_pairs={{0,8},{1,25},{2,10},{3,27},{4,12},{5,29},{6,14},{7,31},{8,16},{9,1... | collective-permute-start | bytes 3145736 | tf_op jit(solution)/shard_map/ppermute | solution.py:39
  105.6 17.9 %collective-permute-start.8 = (bf16[384,1024]{1,0:T(8,128)(2,1)}, bf16[384,1024]{1,0:T(8,128)(2,1)}, u32[]{:S(2)}, u32[]{:S(2)}) collective-permute-start(bf16[384,1024]{1,0:T(8,128)(2,1)} %get-tuple-element.23.own), channel_id=1, source_target_pairs={{0,1},{1,0},{2,3},{3,2},{4,5},{5,4},{6,7},{7,6},{8,9},{9,8},{10,11... | collective-permute-start | bytes 2359304 | tf_op jit(solution)/shard_map/ppermute | solution.py:33
  121.5 23.1 %collective-permute-start.22 = (bf16[384,768]{1,0:T(8,128)(2,1)}, bf16[384,768]{1,0:T(8,128)(2,1)}, u32[]{:S(2)}, u32[]{:S(2)}) collective-permute-start(bf16[384,768]{1,0:T(8,128)(2,1)} %copy-done.2), channel_id=1, source_target_pairs={{0,1},{1,0},{2,3},{3,2},{4,5},{5,4},{6,7},{7,6},{8,9},{9,8},{10,11... | collective-permute-start | bytes 1769480 | tf_op jit(solution)/shard_map/ppermute | solution.py:33
  131.2 4.4 %copy-start.9 = (s32[768]{0:T(1024)S(1)}, s32[768]{0:T(1024)}, u32[]{:S(2)}) copy-start(s32[768]{0:T(1024)} %param.24) | copy-start | bytes 9220
  131.2 5.2 %copy-start.8 = (f32[1024]{0:T(1024)S(1)}, f32[1024]{0:T(1024)}, u32[]{:S(2)}) copy-start(f32[1024]{0:T(1024)} %param.21) | copy-start | bytes 12292
  134.8 1.5 collective-permute-start.21
  136.4 1.4 copy-start.1
  139.1 12.3 %all-to-all-start.1 = ((bf16[16,8,768]{2,1,0:T(8,128)(2,1)}), bf16[16,8,768]{2,1,0:T(8,128)(2,1)S(1)}, u32[]{:S(2)}, u32[]{:S(2)}) async-start(bf16[16,8,768]{2,1,0:T(8,128)(2,1)} %broadcast_in_dim.8), calls=%async_computation.1 | async-start | bytes 393216 | tf_op jit(solution)/shard_map/all_to_all | solution.py:308
  144.6 18.0 %copy-start.11 = (f32[6]{0:T(128)S(1)}, f32[6]{0:T(128)}, u32[]{:S(2)}) copy-start(f32[6]{0:T(128)} %param.25) | copy-start | bytes 76
where the time goes:
time: 165 us; the launch traced here: 163 us
  waiting for transfers between devices  62.7 us (38%)
  starting transfers between devices  52.3 us (32%)
  Pallas kernels  29.1 us (18%)
  blocking collectives  10.1 us (6%)
  local copies, waits for them, and re-layouts  5.63 us (3%)
  other arithmetic  2.9 us (2%)
    pallas_call x16, Pallas kernels, call(): pl.pallas_call(body, out_shape=outs, grid_spec=pltpu.PrefetchScalarGridSp...  29.1 us
    ppermute x6, waiting for transfers between devices, ring(): behind = lax.ppermute(array, AXES, shift_pairs(axis, -1))  19.8 us
    ppermute x6, starting transfers between devices, ring(): far = lax.ppermute(ahead, AXES, shift_pairs(axis, 1))  17.1 us
    ppermute x6, waiting for transfers between devices, ring(): ahead = lax.ppermute(array, AXES, shift_pairs(axis, 1))  16.5 us
    all_to_all x1, waiting for transfers between devices, shards(): lax.all_to_all(jnp.broadcast_to(shard_a[None], (16, 64, 512)), 'dp', 0, 0...  15.5 us
    ppermute x5, starting transfers between devices, swapped(): return lax.ppermute(array, AXES, SWAP)  10.8 us
    all_to_all x1, blocking collectives, shards(): parts = lax.all_to_all(parts.reshape(16, 8, 128), 'dp', 0, 0, tiled=True)  10.1 us
    ppermute x6, starting transfers between devices, ring(): ahead = lax.ppermute(array, AXES, shift_pairs(axis, 1))  9.91 us
  transfers between devices with their start and end apart: 25, of which 8 were waited for; matrix products, arithmetic and copies ran while one was open for 2% of the time, Pallas kernels for 17%

commit v1 on v0

--- a/solution.py
+++ b/solution.py
@@ -77,13 +77,33 @@
     other_out[...] = norm_rows(other[...].astype(F32), gain[...]).astype(BF16)
 
 
-def pack_kernel(up, down, text, scale, out):
-    out[0:64] = up[...]
-    out[64:128] = down[...]
-    out[128:224] = text[:, 0:512]
-    out[224:272, 0:256] = text[0:48, 512:768]
-    out[224:272, 256:512] = text[48:96, 512:768]
-    out[272:288] = scale[...]
+def spread_kernel(joint, output, out):
+    row = jnp.concatenate([joint[0], joint[1], joint[2], output[...]], axis=1)
+    for d in range(16):
+        out[d] = row
+
+
+def pack_kernel(scale, up, down, text, out, sems):
+    copies = [
+        pltpu.make_async_copy(up, out.at[0:64], sems.at[0]),
+        pltpu.make_async_copy(down, out.at[64:128], sems.at[1]),
+        pltpu.make_async_copy(text.at[:, 0:512], out.at[128:224], sems.at[2]),
+        pltpu.make_async_copy(text.at[0:48, 512:768], out.at[224:272, 0:256], sems.at[3]),
+        pltpu.make_async_copy(text.at[48:96, 512:768], out.at[224:272, 256:512], sems.at[4]),
+    ]
+    for copy in copies:
+        copy.start()
+    lane = lax.broadcasted_iota(jnp.int32, (16, 512), 1)
+    row = lax.broadcasted_iota(jnp.int32, (16, 512), 0)
+    value = jnp.where(lane < 64, scale[0], scale[1])
+    high = value.astype(BF16).astype(F32)
+    middle = (value - high).astype(BF16).astype(F32)
+    low = value - high - middle
+    out[272:288] = jnp.where(
+        row == 0, high, jnp.where(row == 1, middle, jnp.where(row == 2, low, 0.0))
+    ).astype(BF16)
+    for copy in copies:
+        copy.wait()
 
 
 def unpack_kernel(m0, m1, m2, m3, ups, downs, texts, scales):
@@ -96,11 +116,6 @@
         scales[r * 8 : (r + 1) * 8] = jnp.broadcast_to(
             jnp.sum(m[272:288, 0:128].astype(F32), axis=0, keepdims=True), (8, 128)
         )
-
-
-def join_kernel(a, b, c, d, out):
-    for r, part in enumerate((a, b, c, d)):
-        out[r * 256 : (r + 1) * 256] = part[...]
 
 
 def interleave_kernel(a, b, c, d, out):
@@ -161,31 +176,38 @@
         mean[side * 8 + 6 : side * 8 + 8, :] = jnp.zeros((2, 512), F32)
 
 
-def down_kernel(place, mean, p0, p1, p2, p3, own, other, weight):
-    for r, piece in enumerate((p0, p1, p2, p3)):
-        for j in range(4):
-            at = pl.multiple_of(place[r * 4 + j] * 64, 64)
-            for k in range(4):
-                weight[pl.ds(at, 64), k * 512 : (k + 1) * 512] = piece[(j * 4 + k) * 64 : (j * 4 + k + 1) * 64, :]
+def down_kernel(place, mean, p0, p1, p2, p3, own, other):
     high, low = split(mean[...])
     both = jnp.concatenate([high, low], axis=0)
-    product = lax.dot_general(both, weight[...], NT, preferred_element_type=F32)
-    product = product[0:16] + product[16:32]
-    own[...] = product[0:8]
-    other[...] = product[8:16]
+    for r, piece in enumerate((p0, p1, p2, p3)):
+        product = jnp.zeros((32, 256), F32)
+        for k in range(4):
+            product = product + lax.dot_general(
+                both[:, k * 512 : (k + 1) * 512],
+                piece[k * 256 : (k + 1) * 256, :],
+                NT,
+                preferred_element_type=F32,
+            )
+        product = product[0:16] + product[16:32]
+        for j in range(4):
+            own[place[r * 4 + j]] = product[0:8, j * 64 : (j + 1) * 64]
+            other[place[r * 4 + j]] = product[8:16, j * 64 : (j + 1) * 64]
 
 
 def final_kernel(pooled, own, other, gain, project, units):
-    total = pooled[...] + own[...] + other[...]
-    normed = norm_rows(total, gain[...]).astype(BF16)
+    feed = jnp.concatenate([own[d] + other[d] for d in range(16)], axis=1)
+    normed = norm_rows(pooled[...] + feed, gain[...]).astype(BF16)
     embedded = jnp.dot(normed, project[...], preferred_element_type=F32)
-    units[...] = (
-        embedded * lax.rsqrt(jnp.sum(embedded * embedded, axis=-1, keepdims=True) + 1e-06)
-    ).astype(BF16)
-
-
-def logits_kernel(units, texts, wanted, ids, out):
-    logits = lax.dot_general(units[...], texts[...], NT, preferred_element_type=F32)
+    unit = (embedded * lax.rsqrt(jnp.sum(embedded * embedded, axis=-1, keepdims=True) + 1e-06)).astype(BF16)
+    for d in range(16):
+        units[d] = unit
+
+
+def logits_kernel(units, texts, texts_other, wanted, ids, out):
+    image = units[...]
+    logits = jnp.concatenate(
+        [lax.dot_general(image, t[...], NT, preferred_element_type=F32) for t in (texts, texts_other)], axis=1
+    )
     highest = jnp.max(logits, axis=1, keepdims=True)
     total = jnp.sum(jnp.exp(logits - highest), axis=1, keepdims=True)
     matched = jnp.sum(jnp.where(wanted[...] == ids[...], logits, 0.0), axis=1, keepdims=True)
@@ -234,15 +256,18 @@
     rows_other = swapped(rows)
     sds = jax.ShapeDtypeStruct
 
-    lanes = jnp.repeat(head_scale, 64)
-    high = lax.reduce_precision(lanes, 8, 7)
-    middle = lax.reduce_precision(lanes - high, 8, 7)
-    low = lanes - high - middle
-    scale_rows = jnp.pad(jnp.stack([high, middle, low]), ((0, 13), (0, 384))).astype(BF16)
-    message = call(pack_kernel, [sds((288, 512), BF16)], [up_weight, down_weight.T, text_bank, scale_rows])[0]
+    spread = call(spread_kernel, [sds((16, 64, 512), BF16)], [jnp.moveaxis(joint_weight, 1, 0), output_weight.T])[0]
+    anywhere = pl.BlockSpec(memory_space=pl.ANY)
+    message = call(
+        pack_kernel,
+        [sds((288, 512), BF16)],
+        [head_scale, up_weight, down_weight.T, text_bank],
+        ins=[anywhere] * 3,
+        scratch=[pltpu.SemaphoreType.DMA((5,))],
+        prefetch=1,
+    )[0]
     messages = ring(message, 2)
-    shard_a = jnp.concatenate([joint_weight.reshape(64, 384), output_weight.T], axis=1)
-    plane_a = lax.all_to_all(jnp.broadcast_to(shard_a[None], (16, 64, 512)), "dp", 0, 0, tiled=True)
+    plane_a = lax.all_to_all(spread, "dp", 0, 0, tiled=True)
     pieces_a = ring(plane_a.reshape(1024, 512), 2)
     first_b, first_c, texts_own, scales = call(
         unpack_kernel,
@@ -250,10 +275,10 @@
         messages,
     )
     second_b = call(interleave_kernel, [sds((1024, 512), BF16)], ring(first_b, 1))[0]
-    second_c = call(join_kernel, [sds((1024, 512), BF16)], ring(first_c, 0))[0]
+    second_c = call(interleave_kernel, [sds((1024, 512), BF16)], ring(first_c, 0))[0]
     pieces_b = ring(second_b, 0)
     pieces_c = ring(second_c, 1)
-    texts = jnp.concatenate([texts_own, swapped(texts_own)], axis=0)
+    texts_other = swapped(texts_own)
 
     gain_row = gain_first.reshape(1, 1024)
     normed_own, normed_other = call(norm_kernel, [sds((384, 1024), BF16)] * 2, [rows, rows_other, gain_row])
@@ -286,16 +311,11 @@
         prefetch=1,
     )[0]
     feed_own, feed_other = call(
-        down_kernel,
-        [sds((8, 1024), F32)] * 2,
-        [by_y_x, mean, *pieces_c],
-        scratch=[pltpu.VMEM((1024, 2048), BF16)],
-        limit=24,
-        prefetch=1,
+        down_kernel, [sds((16, 8, 64), F32)] * 2, [by_y_x, mean, *pieces_c], limit=24, prefetch=1
     )
     units = call(
         final_kernel,
-        [sds((8, 768), BF16)],
+        [sds((16, 8, 768), BF16)],
         [pooled, feed_own, swapped(feed_other), gain_final.reshape(1, 1024), project_weight],
     )[0]
 
@@ -305,8 +325,10 @@
     wanted = lax.dynamic_slice_in_dim(captions.reshape(16, 8, 6), mp, 1, axis=1)[:, 0]
     wanted = jnp.pad(wanted, ((0, 0), (0, 2)), constant_values=-1).reshape(128, 1)
 
-    everyone = lax.all_to_all(jnp.broadcast_to(units[None], (16, 8, 768)), "dp", 0, 0, tiled=True)
-    parts = call(logits_kernel, [sds((128, 128), F32)], [everyone.reshape(128, 768), texts, wanted, ids])[0]
+    everyone = lax.all_to_all(units, "dp", 0, 0, tiled=True)
+    parts = call(
+        logits_kernel, [sds((128, 128), F32)], [everyone.reshape(128, 768), texts_own, texts_other, wanted, ids]
+    )[0]
     parts = lax.all_to_all(parts.reshape(16, 8, 128), "dp", 0, 0, tiled=True)
     loss = call(loss_kernel, [sds((8, 128), F32)], [parts])[0]
     return loss[0:6, 0] - reference_loss

time: 165 us -> 162 us (0.982)
  blocking collectives: 10.1 us -> 33.6 us
  waiting for transfers between devices: 62.7 us -> 48.4 us
  starting transfers between devices: 52.3 us -> 45.1 us
  local copies, waits for them, and re-layouts: 5.63 us -> 2.99 us
  other arithmetic: 2.9 us -> 0.83 us
    all_to_all x0 -> x1, blocking collectives: none -> 23.4 us  [shards(): plane_a = lax.all_to_all(spread, 'dp', 0, 0, tiled=True)]
    all_to_all x2 -> x1, waiting for transfers between devices: 21 us -> 6.58 us  [shards(): everyone = lax.all_to_all(units, 'dp', 0, 0, tiled=True)]
    all_to_all x2 -> x1, starting transfers between devices: 12.9 us -> 5.87 us  [shards(): everyone = lax.all_to_all(units, 'dp', 0, 0, tiled=True)]
    concatenate x2 -> x0, other arithmetic: 2.05 us -> none  [the longest x1 1.32 us: shards(): texts = jnp.concatenate([texts_own, swapped(texts_own)], axis=0)]
    broadcast_in_dim x3 -> x0, local copies, waits for them, and re-layouts: 1.88 us -> none  [the longest x1 1.1 us: shards(): jnp.broadcast_to(shard_a[None], (16, 64, 512))]
    pallas_call x16 -> x17, Pallas kernels: 29.1 us -> 29.3 us  [call(): pl.pallas_call(body, out_shape=outs, grid_spec=pltpu.PrefetchScalarGridSp...]
  transfers between devices with their start and end apart: 25 -> 24, of which waited for: 8 -> 7; matrix products, arithmetic and copies ran while one was open for 2% -> 0% of each run, Pallas kernels for 17% -> 17%
where the time goes in v1:
time: 162 us; the launch traced here: 160 us
  waiting for transfers between devices  48.4 us (30%)
  starting transfers between devices  45.1 us (28%)
  blocking collectives  33.6 us (21%)
  Pallas kernels  29.3 us (18%)
  local copies, waits for them, and re-layouts  2.99 us (2%)
    pallas_call x17, Pallas kernels, call(): pl.pallas_call(body, out_shape=outs, grid_spec=pltpu.PrefetchScalarGridSp...  29.3 us
    all_to_all x1, blocking collectives, shards(): plane_a = lax.all_to_all(spread, 'dp', 0, 0, tiled=True)  23.4 us
    ppermute x6, waiting for transfers between devices, ring(): behind = lax.ppermute(array, AXES, shift_pairs(axis, -1))  20.8 us
    ppermute x6, starting transfers between devices, ring(): far = lax.ppermute(ahead, AXES, shift_pairs(axis, 1))  15.9 us
    ppermute x6, waiting for transfers between devices, ring(): ahead = lax.ppermute(array, AXES, shift_pairs(axis, 1))  15.7 us
    ppermute x5, starting transfers between devices, swapped(): return lax.ppermute(array, AXES, SWAP)  11.1 us
    all_to_all x1, blocking collectives, shards(): parts = lax.all_to_all(parts.reshape(16, 8, 128), 'dp', 0, 0, tiled=True)  10.1 us
    ppermute x6, starting transfers between devices, ring(): ahead = lax.ppermute(array, AXES, shift_pairs(axis, 1))  9.87 us
  transfers between devices with their start and end apart: 24, of which 7 were waited for; matrix products, arithmetic and copies ran while one was open for 0% of the time, Pallas kernels for 17%

profile of v1, /device:TPU:1, one launch (start us, length us, event | category | flops | bytes accessed | tf_op | source)
XLA Modules:
  0.0 160.4 jit_solution(12776667589911506973)
XLA Ops:
  0.0 0.8 copy-done.7
  0.8 0.7 copy-done.8
  1.5 0.1 shard_map.128
  1.6 23.4 %all_to_all.15 = bf16[16,64,512]{2,1,0:T(8,128)(2,1)S(1)} all-to-all(bf16[16,64,512]{2,1,0:T(8,128)(2,1)S(1)} %shard_map.128), channel_id=1, replica_groups=mesh['dp'=16,'mp'=8] {'dp'}, dimensions={0} | all-to-all | bytes 2097152 | tf_op jit(solution)/shard_map/all_to_all | solution.py:270
  25.1 3.8 %collective-permute-start.4 = (bf16[1024,512]{1,0:T(8,128)(2,1)S(1)}, bf16[1024,512]{1,0:T(8,128)(2,1)S(1)}, u32[]{:S(2)}, u32[]{:S(2)}) collective-permute-start(bf16[1024,512]{1,0:T(8,128)(2,1)S(1)} %bitcast.16), channel_id=1, source_target_pairs={{0,2},{1,7},{2,4},{3,1},{4,6},{5,3},{6,0},{7,5},{8,10},{9,15},{10,... | collective-permute-start | bytes 3145736 | tf_op jit(solution)/shard_map/ppermute | solution.py:37
  28.9 0.8 shard_map.129.m0
  29.7 0.2 collective-permute-start.1
  29.9 1.3 collective-permute-start.2
  31.2 15.7 %collective-permute-done.1.m1 = bf16[288,512]{1,0:T(8,128)(2,1)S(1)} collective-permute-done((bf16[288,512]{1,0:T(8,128)(2,1)S(1)}, bf16[288,512]{1,0:T(8,128)(2,1)S(1)}, u32[]{:S(2)}, u32[]{:S(2)}) %collective-permute-start.1) | collective-permute-done | bytes 294944 | tf_op jit(solution)/shard_map/ppermute | solution.py:37
  46.9 3.1 %collective-permute-start.3 = (bf16[288,512]{1,0:T(8,128)(2,1)S(1)}, bf16[288,512]{1,0:T(8,128)(2,1)S(1)}, u32[]{:S(2)}, u32[]{:S(2)}) collective-permute-start(bf16[288,512]{1,0:T(8,128)(2,1)S(1)} %collective-permute-done.1.m1), channel_id=1, source_target_pairs={{0,2},{1,7},{2,4},{3,1},{4,6},{5,3},{6,0},{7,5},{8,10},{9,15},{10,... | collective-permute-start | bytes 884744 | tf_op jit(solution)/shard_map/ppermute | solution.py:39
  50.0 3.7 %collective-permute-done.3.m3 = bf16[288,512]{1,0:T(8,128)(2,1)S(1)} collective-permute-done((bf16[288,512]{1,0:T(8,128)(2,1)S(1)}, bf16[288,512]{1,0:T(8,128)(2,1)S(1)}, u32[]{:S(2)}, u32[]{:S(2)}) %collective-permute-start.3) | collective-permute-done | bytes 294944 | tf_op jit(solution)/shard_map/ppermute | solution.py:39
  53.8 0.8 copy-done.2
  54.6 0.6 collective-permute-start.9
  55.2 0.8 collective-permute-start.10
  56.1 3.1 %collective-permute-start.6 = (bf16[1024,512]{1,0:T(8,128)(2,1)S(1)}, bf16[1024,512]{1,0:T(8,128)(2,1)S(1)}, u32[]{:S(2)}, u32[]{:S(2)}) collective-permute-start(bf16[1024,512]{1,0:T(8,128)(2,1)S(1)} %collective-permute-done.4.piece.p1), channel_id=1, source_target_pairs={{0,2},{1,7},{2,4},{3,1},{4,6},{5,3},{6,0},{7,5},{8,10},{9,15},{10,... | collective-permute-start | bytes 3145736 | tf_op jit(solution)/shard_map/ppermute | solution.py:39
  59.2 0.9 collective-permute-start.15
  60.1 1.6 collective-permute-start.11
  61.7 6.6 %collective-permute-start = (bf16[384,1024]{1,0:T(8,128)(2,1)S(1)}, bf16[384,1024]{1,0:T(8,128)(2,1)S(1)}, u32[]{:S(2)}, u32[]{:S(2)}) collective-permute-start(bf16[384,1024]{1,0:T(8,128)(2,1)S(1)} %bitcast.20), channel_id=1, source_target_pairs={{0,1},{1,0},{2,3},{3,2},{4,5},{5,4},{6,7},{7,6},{8,9},{9,8},{10,11... | collective-permute-start | bytes 2359304 | tf_op jit(solution)/shard_map/ppermute | solution.py:33
  68.2 0.2 collective-permute-start.16
  68.4 2.5 %collective-permute-start.17 = (bf16[256,512]{1,0:T(8,128)(2,1)S(1)}, bf16[256,512]{1,0:T(8,128)(2,1)S(1)}, u32[]{:S(2)}, u32[]{:S(2)}) collective-permute-start(bf16[256,512]{1,0:T(8,128)(2,1)S(1)} %collective-permute-done.15.b), channel_id=1, source_target_pairs={{0,32},{1,97},{2,34},{3,99},{4,36},{5,101},{6,38},{7,103},{8,40},{... | collective-permute-start | bytes 786440 | tf_op jit(solution)/shard_map/ppermute | solution.py:39
  71.0 4.0 %collective-permute-done.16.c = bf16[256,512]{1,0:T(8,128)(2,1)S(1)} collective-permute-done((bf16[256,512]{1,0:T(8,128)(2,1)S(1)}, bf16[256,512]{1,0:T(8,128)(2,1)S(1)}, u32[]{:S(2)}, u32[]{:S(2)}) %collective-permute-start.16) | collective-permute-done | bytes 262176 | tf_op jit(solution)/shard_map/ppermute | solution.py:38
  75.0 0.8 collective-permute-done.17.d
  75.8 4.4 %collective-permute-start.18 = (bf16[1024,512]{1,0:T(8,128)(2,1)S(1)}, bf16[1024,512]{1,0:T(8,128)(2,1)S(1)}, u32[]{:S(2)}, u32[]{:S(2)}) collective-permute-start(bf16[1024,512]{1,0:T(8,128)(2,1)S(1)} %shard_map.139.p0), channel_id=1, source_target_pairs={{0,8},{1,25},{2,10},{3,27},{4,12},{5,29},{6,14},{7,31},{8,16},{9,1... | collective-permute-start | bytes 3145736 | tf_op jit(solution)/shard_map/ppermute | solution.py:37
  80.2 1.0 shard_map.127
  81.2 2.5 %shard_map.131.h0 = bf16[768,128]{1,0:T(8,128)(2,1)S(1)} custom-call(bf16[384,1024]{1,0:T(8,128)(2,1)S(1)} %get-tuple-element.17.own, bf16[384,1024]{1,0:T(8,128)(2,1)S(1)} %get-tuple-element.18.other, bf16[1024,512]{1,0:T(8,128)(2,1)S(1)} %bitcast.18, f32[32,128]{1,0:T(8,128)S(1)} %get-tuple-element.19.scales), custom_call_target="tpu_custom_call" | custom-call | tf_op jit(solution)/shard_map/pallas_call | solution.py:48
  83.7 2.5 %shard_map.132.h1 = bf16[768,128]{1,0:T(8,128)(2,1)S(1)} custom-call(bf16[384,1024]{1,0:T(8,128)(2,1)S(1)} %get-tuple-element.17.own, bf16[384,1024]{1,0:T(8,128)(2,1)S(1)} %get-tuple-element.18.other, bf16[1024,512]{1,0:T(8,128)(2,1)S(1)} %collective-permute-done.4.piece.p1, f32[32,128]{1,0:T(8,128)S(1)} %get-tuple-element.19.scales), custom_call_target="tpu_custom_call" | custom-call | tf_op jit(solution)/shard_map/pallas_call | solution.py:48
  86.3 2.5 %shard_map.133.h2 = bf16[768,128]{1,0:T(8,128)(2,1)S(1)} custom-call(bf16[384,1024]{1,0:T(8,128)(2,1)S(1)} %get-tuple-element.17.own, bf16[384,1024]{1,0:T(8,128)(2,1)S(1)} %get-tuple-element.18.other, bf16[1024,512]{1,0:T(8,128)(2,1)S(1)} %collective-permute-done.5.piece.p2, f32[32,128]{1,0:T(8,128)S(1)} %get-tuple-element.19.scales), custom_call_target="tpu_custom_call" | custom-call | tf_op jit(solution)/shard_map/pallas_call | solution.py:48
  88.8 2.5 %shard_map.134.h3 = bf16[768,128]{1,0:T(8,128)(2,1)S(1)} custom-call(bf16[384,1024]{1,0:T(8,128)(2,1)S(1)} %get-tuple-element.17.own, bf16[384,1024]{1,0:T(8,128)(2,1)S(1)} %get-tuple-element.18.other, bf16[1024,512]{1,0:T(8,128)(2,1)S(1)} %collective-permute-done.6.piece.p3, f32[32,128]{1,0:T(8,128)S(1)} %get-tuple-element.19.scales), custom_call_target="tpu_custom_call" | custom-call | tf_op jit(solution)/shard_map/pallas_call | solution.py:48
  91.4 1.1 shard_map.135
  92.4 1.9 %collective-permute-start.7 = (bf16[384,1024]{1,0:T(8,128)(2,1)S(1)}, bf16[384,1024]{1,0:T(8,128)(2,1)S(1)}, u32[]{:S(2)}, u32[]{:S(2)}) collective-permute-start(bf16[384,1024]{1,0:T(8,128)(2,1)S(1)} %get-tuple-element.21), channel_id=1, source_target_pairs={{0,1},{1,0},{2,3},{3,2},{4,5},{5,4},{6,7},{7,6},{8,9},{9,8},{10,11... | collective-permute-start | bytes 2359304 | tf_op jit(solution)/shard_map/ppermute | solution.py:33
  94.4 2.7 %collective-permute-start.14 = (bf16[1024,512]{1,0:T(8,128)(2,1)}, bf16[1024,512]{1,0:T(8,128)(2,1)}, u32[]{:S(2)}, u32[]{:S(2)}) collective-permute-start(bf16[1024,512]{1,0:T(8,128)(2,1)} %collective-permute-done.12.p1), channel_id=1, source_target_pairs={{0,32},{1,97},{2,34},{3,99},{4,36},{5,101},{6,38},{7,103},{8,40},{... | collective-permute-start | bytes 3145736 | tf_op jit(solution)/shard_map/ppermute | solution.py:39
  97.0 2.9 %collective-permute-start.20 = (bf16[1024,512]{1,0:T(8,128)(2,1)S(1)}, bf16[1024,512]{1,0:T(8,128)(2,1)}, u32[]{:S(2)}, u32[]{:S(2)}) collective-permute-start(bf16[1024,512]{1,0:T(8,128)(2,1)S(1)} %collective-permute-done.18.p1), channel_id=1, source_target_pairs={{0,8},{1,25},{2,10},{3,27},{4,12},{5,29},{6,14},{7,31},{8,16},{9,1... | collective-permute-start | bytes 3145736 | tf_op jit(solution)/shard_map/ppermute | solution.py:39
  100.0 1.6 shard_map.136
  101.7 16.8 %collective-permute-done.13.p2 = bf16[1024,512]{1,0:T(8,128)(2,1)} collective-permute-done((bf16[1024,512]{1,0:T(8,128)(2,1)S(1)}, bf16[1024,512]{1,0:T(8,128)(2,1)}, u32[]{:S(2)}, u32[]{:S(2)}) %collective-permute-start.13) | collective-permute-done | bytes 1048608 | tf_op jit(solution)/shard_map/ppermute | solution.py:38
  118.5 1.9 %collective-permute-start.22 = (bf16[384,768]{1,0:T(8,128)(2,1)}, bf16[384,768]{1,0:T(8,128)(2,1)}, u32[]{:S(2)}, u32[]{:S(2)}) collective-permute-start(bf16[384,768]{1,0:T(8,128)(2,1)} %copy-done.2), channel_id=1, source_target_pairs={{0,1},{1,0},{2,3},{3,2},{4,5},{5,4},{6,7},{7,6},{8,9},{9,8},{10,11... | collective-permute-start | bytes 1769480 | tf_op jit(solution)/shard_map/ppermute | solution.py:33
  120.6 7.7 %shard_map.138.mean = f32[16,2048]{1,0:T(8,128)S(1)} custom-call(s32[16]{0:T(128)S(1)} %add.220.place, bf16[384,1024]{1,0:T(8,128)(2,1)} %get-tuple-element.23.own, bf16[384,1024]{1,0:T(8,128)(2,1)} %collective-permute-done.8.other, bf16[1024,512]{1,0:T(8,128)(2,1)S(1)} %shard_map.137.p0, bf16[1024,512]{1,0:T(8,128)(2,1)} %collective-permute-done.12.p1, ...), custom_call_target="tpu_custom_call" | custom-call | tf_op jit(solution)/shard_map/pallas_call | solution.py:48
  128.4 3.4 %shard_map.140 = (f32[16,8,64]{2,1,0:T(8,128)S(1)}, f32[16,8,64]{2,1,0:T(8,128)S(1)}) custom-call(s32[16]{0:T(128)S(1)} %add.216.place, f32[16,2048]{1,0:T(8,128)S(1)} %shard_map.138.mean, bf16[1024,512]{1,0:T(8,128)(2,1)S(1)} %shard_map.139.p0, bf16[1024,512]{1,0:T(8,128)(2,1)S(1)} %collective-permute-done.18.p1, ...), custom_call_target="tpu_custom_call" | custom-call | tf_op jit(solution)/shard_map/pallas_call | solution.py:48
  131.9 0.7 collective-permute-start.21
  132.6 0.8 collective-permute-done.21.other
  133.5 1.3 shard_map.141
  134.8 5.9 %all-to-all-start.1 = ((bf16[16,8,768]{2,1,0:T(8,128)(2,1)}), bf16[16,8,768]{2,1,0:T(8,128)(2,1)S(1)}, u32[]{:S(2)}, u32[]{:S(2)}) async-start(bf16[16,8,768]{2,1,0:T(8,128)(2,1)} %shard_map.141), calls=%async_computation.1 | async-start | bytes 393216 | tf_op jit(solution)/shard_map/all_to_all | solution.py:328
  140.8 0.1 reshape.273
  141.1 6.6 %all-to-all-done.1 = bf16[16,8,768]{2,1,0:T(8,128)(2,1)S(1)} async-done(((bf16[16,8,768]{2,1,0:T(8,128)(2,1)}), bf16[16,8,768]{2,1,0:T(8,128)(2,1)S(1)}, u32[]{:S(2)}, u32[]{:S(2)}) %all-to-all-start.1) | async-done | bytes 196640 | tf_op jit(solution)/shard_map/all_to_all | solution.py:328
  147.7 1.7 %shard_map.142 = f32[128,128]{1,0:T(8,128)S(1)} custom-call(bf16[128,768]{1,0:T(8,128)(2,1)S(1)} %bitcast.23, bf16[384,768]{1,0:T(8,128)(2,1)S(1)} %copy-done.3, bf16[384,768]{1,0:T(8,128)(2,1)} %collective-permute-done.22.texts_other, s32[128,1]{1,0:T(8,128)S(1)} %reshape.276.wanted, s32[1,768]{1,0:T(1,128)S(1)} %add.237.ids), custom_call_target="tpu_custom_call" | custom-call | tf_op jit(solution)/shard_map/pallas_call | solution.py:48
  149.4 10.1 %all_to_all.16.parts = f32[16,8,128]{2,1,0:T(8,128)S(1)} all-to-all(f32[16,8,128]{2,1,0:T(8,128)S(1)} %bitcast.24), channel_id=1, replica_groups=mesh['dp'=16,'mp'=8] {'dp'}, dimensions={0} | all-to-all | bytes 131072 | tf_op jit(solution)/shard_map/all_to_all | solution.py:332
  159.5 0.2 shard_map.143
  159.7 0.1 slice_reduce_fusion
  159.9 0.5 sub.27
  (63 shorter events, 1.0 us)
Async XLA Ops:
  0.0 0.8 copy-start.7
  0.8 0.7 copy-start.8
  1.5 27.3 %copy-start.4 = (bf16[96,768]{1,0:T(8,128)(2,1)S(1)}, bf16[96,768]{1,0:T(8,128)(2,1)}, u32[]{:S(2)}) copy-start(bf16[96,768]{1,0:T(8,128)(2,1)} %text.1) | copy-start | bytes 442372
  1.5 27.3 %copy-start.5 = (bf16[64,512]{1,0:T(8,128)(2,1)S(1)}, bf16[64,512]{1,0:T(8,128)(2,1)}, u32[]{:S(2)}) copy-start(bf16[64,512]{1,0:T(8,128)(2,1)} %up.1) | copy-start | bytes 196612
  1.5 27.3 %copy-start.6 = (bf16[512,64]{0,1:T(8,128)(2,1)S(1)}, bf16[512,64]{0,1:T(8,128)(2,1)}, u32[]{:S(2)}) copy-start(bf16[512,64]{0,1:T(8,128)(2,1)} %param.20) | copy-start | bytes 196612
  1.5 27.3 %copy-start.12 = (f32[2]{0:T(128)S(1)}, f32[2]{0:T(128)}, u32[]{:S(2)}) copy-start(f32[2]{0:T(128)} %scale.1) | copy-start | bytes 28
  1.6 60.0 %copy-start = (bf16[6,64,1024]{2,1,0:T(8,128)(2,1)S(1)}, bf16[6,64,1024]{2,1,0:T(8,128)(2,1)}, u32[]{:S(2)}) copy-start(bf16[6,64,1024]{2,1,0:T(8,128)(2,1)} %param.13) | copy-start | bytes 2359300
  25.1 31.0 %collective-permute-start.4 = (bf16[1024,512]{1,0:T(8,128)(2,1)S(1)}, bf16[1024,512]{1,0:T(8,128)(2,1)S(1)}, u32[]{:S(2)}, u32[]{:S(2)}) collective-permute-start(bf16[1024,512]{1,0:T(8,128)(2,1)S(1)} %bitcast.16), channel_id=1, source_target_pairs={{0,2},{1,7},{2,4},{3,1},{4,6},{5,3},{6,0},{7,5},{8,10},{9,15},{10,... | collective-permute-start | bytes 3145736 | tf_op jit(solution)/shard_map/ppermute | solution.py:37
  29.7 17.2 %collective-permute-start.1 = (bf16[288,512]{1,0:T(8,128)(2,1)S(1)}, bf16[288,512]{1,0:T(8,128)(2,1)S(1)}, u32[]{:S(2)}, u32[]{:S(2)}) collective-permute-start(bf16[288,512]{1,0:T(8,128)(2,1)S(1)} %shard_map.129.m0), channel_id=1, source_target_pairs={{0,2},{1,7},{2,4},{3,1},{4,6},{5,3},{6,0},{7,5},{8,10},{9,15},{10,... | collective-permute-start | bytes 884744 | tf_op jit(solution)/shard_map/ppermute | solution.py:37
  29.9 20.2 %collective-permute-start.2 = (bf16[288,512]{1,0:T(8,128)(2,1)S(1)}, bf16[288,512]{1,0:T(8,128)(2,1)S(1)}, u32[]{:S(2)}, u32[]{:S(2)}) collective-permute-start(bf16[288,512]{1,0:T(8,128)(2,1)S(1)} %shard_map.129.m0), channel_id=1, source_target_pairs={{0,6},{1,3},{2,0},{3,5},{4,2},{5,7},{6,4},{7,1},{8,14},{9,11},{10,... | collective-permute-start | bytes 884744 | tf_op jit(solution)/shard_map/ppermute | solution.py:38
  46.9 6.8 %collective-permute-start.3 = (bf16[288,512]{1,0:T(8,128)(2,1)S(1)}, bf16[288,512]{1,0:T(8,128)(2,1)S(1)}, u32[]{:S(2)}, u32[]{:S(2)}) collective-permute-start(bf16[288,512]{1,0:T(8,128)(2,1)S(1)} %collective-permute-done.1.m1), channel_id=1, source_target_pairs={{0,2},{1,7},{2,4},{3,1},{4,6},{5,3},{6,0},{7,5},{8,10},{9,15},{10,... | collective-permute-start | bytes 884744 | tf_op jit(solution)/shard_map/ppermute | solution.py:39
  53.8 0.8 copy-start.2
  54.6 5.5 %collective-permute-start.9 = (bf16[256,512]{1,0:T(8,128)(2,1)S(1)}, bf16[256,512]{1,0:T(8,128)(2,1)S(1)}, u32[]{:S(2)}, u32[]{:S(2)}) collective-permute-start(bf16[256,512]{1,0:T(8,128)(2,1)S(1)} %get-tuple-element.24.a), channel_id=1, source_target_pairs={{0,8},{1,25},{2,10},{3,27},{4,12},{5,29},{6,14},{7,31},{8,16},{9,1... | collective-permute-start | bytes 786440 | tf_op jit(solution)/shard_map/ppermute | solution.py:37
  55.2 6.4 %collective-permute-start.10 = (bf16[256,512]{1,0:T(8,128)(2,1)S(1)}, bf16[256,512]{1,0:T(8,128)(2,1)S(1)}, u32[]{:S(2)}, u32[]{:S(2)}) collective-permute-start(bf16[256,512]{1,0:T(8,128)(2,1)S(1)} %get-tuple-element.24.a), channel_id=1, source_target_pairs={{0,24},{1,9},{2,26},{3,11},{4,28},{5,13},{6,30},{7,15},{8,0},{9,17... | collective-permute-start | bytes 786440 | tf_op jit(solution)/shard_map/ppermute | solution.py:38
  56.1 30.2 %collective-permute-start.5 = (bf16[1024,512]{1,0:T(8,128)(2,1)S(1)}, bf16[1024,512]{1,0:T(8,128)(2,1)S(1)}, u32[]{:S(2)}, u32[]{:S(2)}) collective-permute-start(bf16[1024,512]{1,0:T(8,128)(2,1)S(1)} %bitcast.17), channel_id=1, source_target_pairs={{0,6},{1,3},{2,0},{3,5},{4,2},{5,7},{6,4},{7,1},{8,14},{9,11},{10,... | collective-permute-start | bytes 3145736 | tf_op jit(solution)/shard_map/ppermute | solution.py:38
  56.1 32.8 %collective-permute-start.6 = (bf16[1024,512]{1,0:T(8,128)(2,1)S(1)}, bf16[1024,512]{1,0:T(8,128)(2,1)S(1)}, u32[]{:S(2)}, u32[]{:S(2)}) collective-permute-start(bf16[1024,512]{1,0:T(8,128)(2,1)S(1)} %collective-permute-done.4.piece.p1), channel_id=1, source_target_pairs={{0,2},{1,7},{2,4},{3,1},{4,6},{5,3},{6,0},{7,5},{8,10},{9,15},{10,... | collective-permute-start | bytes 3145736 | tf_op jit(solution)/shard_map/ppermute | solution.py:39
  59.2 9.0 %collective-permute-start.15 = (bf16[256,512]{1,0:T(8,128)(2,1)S(1)}, bf16[256,512]{1,0:T(8,128)(2,1)S(1)}, u32[]{:S(2)}, u32[]{:S(2)}) collective-permute-start(bf16[256,512]{1,0:T(8,128)(2,1)S(1)} %get-tuple-element.25.a), channel_id=1, source_target_pairs={{0,32},{1,97},{2,34},{3,99},{4,36},{5,101},{6,38},{7,103},{8,40},{... | collective-permute-start | bytes 786440 | tf_op jit(solution)/shard_map/ppermute | solution.py:37
  60.1 8.3 %collective-permute-start.11 = (bf16[256,512]{1,0:T(8,128)(2,1)S(1)}, bf16[256,512]{1,0:T(8,128)(2,1)S(1)}, u32[]{:S(2)}, u32[]{:S(2)}) collective-permute-start(bf16[256,512]{1,0:T(8,128)(2,1)S(1)} %collective-permute-done.9.b), channel_id=1, source_target_pairs={{0,8},{1,25},{2,10},{3,27},{4,12},{5,29},{6,14},{7,31},{8,16},{9,1... | collective-permute-start | bytes 786440 | tf_op jit(solution)/shard_map/ppermute | solution.py:39
  61.7 18.5 %collective-permute-start = (bf16[384,1024]{1,0:T(8,128)(2,1)S(1)}, bf16[384,1024]{1,0:T(8,128)(2,1)S(1)}, u32[]{:S(2)}, u32[]{:S(2)}) collective-permute-start(bf16[384,1024]{1,0:T(8,128)(2,1)S(1)} %bitcast.20), channel_id=1, source_target_pairs={{0,1},{1,0},{2,3},{3,2},{4,5},{5,4},{6,7},{7,6},{8,9},{9,8},{10,11... | collective-permute-start | bytes 2359304 | tf_op jit(solution)/shard_map/ppermute | solution.py:33
  68.2 6.7 %collective-permute-start.16 = (bf16[256,512]{1,0:T(8,128)(2,1)S(1)}, bf16[256,512]{1,0:T(8,128)(2,1)S(1)}, u32[]{:S(2)}, u32[]{:S(2)}) collective-permute-start(bf16[256,512]{1,0:T(8,128)(2,1)S(1)} %get-tuple-element.25.a), channel_id=1, source_target_pairs={{0,96},{1,33},{2,98},{3,35},{4,100},{5,37},{6,102},{7,39},{8,104},... | collective-permute-start | bytes 786440 | tf_op jit(solution)/shard_map/ppermute | solution.py:38
  68.4 7.3 %collective-permute-start.17 = (bf16[256,512]{1,0:T(8,128)(2,1)S(1)}, bf16[256,512]{1,0:T(8,128)(2,1)S(1)}, u32[]{:S(2)}, u32[]{:S(2)}) collective-permute-start(bf16[256,512]{1,0:T(8,128)(2,1)S(1)} %collective-permute-done.15.b), channel_id=1, source_target_pairs={{0,32},{1,97},{2,34},{3,99},{4,36},{5,101},{6,38},{7,103},{8,40},{... | collective-permute-start | bytes 786440 | tf_op jit(solution)/shard_map/ppermute | solution.py:39
  71.0 9.2 %copy-start.9 = (f32[1024]{0:T(1024)S(1)}, f32[1024]{0:T(1024)}, u32[]{:S(2)}) copy-start(f32[1024]{0:T(1024)} %param.14) | copy-start | bytes 12292
  75.0 19.4 %collective-permute-start.12 = (bf16[1024,512]{1,0:T(8,128)(2,1)S(1)}, bf16[1024,512]{1,0:T(8,128)(2,1)}, u32[]{:S(2)}, u32[]{:S(2)}) collective-permute-start(bf16[1024,512]{1,0:T(8,128)(2,1)S(1)} %shard_map.137.p0), channel_id=1, source_target_pairs={{0,32},{1,97},{2,34},{3,99},{4,36},{5,101},{6,38},{7,103},{8,40},{... | collective-permute-start | bytes 3145736 | tf_op jit(solution)/shard_map/ppermute | solution.py:37
  75.8 21.2 %collective-permute-start.18 = (bf16[1024,512]{1,0:T(8,128)(2,1)S(1)}, bf16[1024,512]{1,0:T(8,128)(2,1)S(1)}, u32[]{:S(2)}, u32[]{:S(2)}) collective-permute-start(bf16[1024,512]{1,0:T(8,128)(2,1)S(1)} %shard_map.139.p0), channel_id=1, source_target_pairs={{0,8},{1,25},{2,10},{3,27},{4,12},{5,29},{6,14},{7,31},{8,16},{9,1... | collective-permute-start | bytes 3145736 | tf_op jit(solution)/shard_map/ppermute | solution.py:37
  91.4 8.6 %copy-start.10 = (f32[1024]{0:T(1024)S(1)}, f32[1024]{0:T(1024)}, u32[]{:S(2)}) copy-start(f32[1024]{0:T(1024)} %param.18) | copy-start | bytes 12292
  92.4 7.5 %collective-permute-start.7 = (bf16[384,1024]{1,0:T(8,128)(2,1)S(1)}, bf16[384,1024]{1,0:T(8,128)(2,1)S(1)}, u32[]{:S(2)}, u32[]{:S(2)}) collective-permute-start(bf16[384,1024]{1,0:T(8,128)(2,1)S(1)} %get-tuple-element.21), channel_id=1, source_target_pairs={{0,1},{1,0},{2,3},{3,2},{4,5},{5,4},{6,7},{7,6},{8,9},{9,8},{10,11... | collective-permute-start | bytes 2359304 | tf_op jit(solution)/shard_map/ppermute | solution.py:33
  94.4 24.1 %collective-permute-start.13 = (bf16[1024,512]{1,0:T(8,128)(2,1)S(1)}, bf16[1024,512]{1,0:T(8,128)(2,1)}, u32[]{:S(2)}, u32[]{:S(2)}) collective-permute-start(bf16[1024,512]{1,0:T(8,128)(2,1)S(1)} %shard_map.137.p0), channel_id=1, source_target_pairs={{0,96},{1,33},{2,98},{3,35},{4,100},{5,37},{6,102},{7,39},{8,104},... | collective-permute-start | bytes 3145736 | tf_op jit(solution)/shard_map/ppermute | solution.py:38
  94.4 26.3 %collective-permute-start.14 = (bf16[1024,512]{1,0:T(8,128)(2,1)}, bf16[1024,512]{1,0:T(8,128)(2,1)}, u32[]{:S(2)}, u32[]{:S(2)}) collective-permute-start(bf16[1024,512]{1,0:T(8,128)(2,1)} %collective-permute-done.12.p1), channel_id=1, source_target_pairs={{0,32},{1,97},{2,34},{3,99},{4,36},{5,101},{6,38},{7,103},{8,40},{... | collective-permute-start | bytes 3145736 | tf_op jit(solution)/shard_map/ppermute | solution.py:39
  97.0 31.3 %collective-permute-start.19 = (bf16[1024,512]{1,0:T(8,128)(2,1)S(1)}, bf16[1024,512]{1,0:T(8,128)(2,1)}, u32[]{:S(2)}, u32[]{:S(2)}) collective-permute-start(bf16[1024,512]{1,0:T(8,128)(2,1)S(1)} %shard_map.139.p0), channel_id=1, source_target_pairs={{0,24},{1,9},{2,26},{3,11},{4,28},{5,13},{6,30},{7,15},{8,0},{9,17... | collective-permute-start | bytes 3145736 | tf_op jit(solution)/shard_map/ppermute | solution.py:38
  97.0 31.3 %collective-permute-start.20 = (bf16[1024,512]{1,0:T(8,128)(2,1)S(1)}, bf16[1024,512]{1,0:T(8,128)(2,1)}, u32[]{:S(2)}, u32[]{:S(2)}) collective-permute-start(bf16[1024,512]{1,0:T(8,128)(2,1)S(1)} %collective-permute-done.18.p1), channel_id=1, source_target_pairs={{0,8},{1,25},{2,10},{3,27},{4,12},{5,29},{6,14},{7,31},{8,16},{9,1... | collective-permute-start | bytes 3145736 | tf_op jit(solution)/shard_map/ppermute | solution.py:39
  101.6 19.1 %collective-permute-start.8 = (bf16[384,1024]{1,0:T(8,128)(2,1)}, bf16[384,1024]{1,0:T(8,128)(2,1)}, u32[]{:S(2)}, u32[]{:S(2)}) collective-permute-start(bf16[384,1024]{1,0:T(8,128)(2,1)} %get-tuple-element.23.own), channel_id=1, source_target_pairs={{0,1},{1,0},{2,3},{3,2},{4,5},{5,4},{6,7},{7,6},{8,9},{9,8},{10,11... | collective-permute-start | bytes 2359304 | tf_op jit(solution)/shard_map/ppermute | solution.py:33
  118.5 22.6 %collective-permute-start.22 = (bf16[384,768]{1,0:T(8,128)(2,1)}, bf16[384,768]{1,0:T(8,128)(2,1)}, u32[]{:S(2)}, u32[]{:S(2)}) collective-permute-start(bf16[384,768]{1,0:T(8,128)(2,1)} %copy-done.2), channel_id=1, source_target_pairs={{0,1},{1,0},{2,3},{3,2},{4,5},{5,4},{6,7},{7,6},{8,9},{9,8},{10,11... | collective-permute-start | bytes 1769480 | tf_op jit(solution)/shard_map/ppermute | solution.py:33
  128.3 5.1 %copy-start.1 = (bf16[1024,768]{1,0:T(8,128)(2,1)S(1)}, bf16[1024,768]{1,0:T(8,128)(2,1)}, u32[]{:S(2)}) copy-start(bf16[1024,768]{1,0:T(8,128)(2,1)} %project.1) | copy-start | bytes 4718596
  128.4 5.1 %copy-start.11 = (f32[1024]{0:T(1024)S(1)}, f32[1024]{0:T(1024)}, u32[]{:S(2)}) copy-start(f32[1024]{0:T(1024)} %param.21) | copy-start | bytes 12292
  131.8 9.0 %copy-start.13 = (s32[768]{0:T(1024)S(1)}, s32[768]{0:T(1024)}, u32[]{:S(2)}) copy-start(s32[768]{0:T(1024)} %param.24) | copy-start | bytes 9220
  131.8 15.8 %copy-start.3 = (bf16[384,768]{1,0:T(8,128)(2,1)S(1)}, bf16[384,768]{1,0:T(8,128)(2,1)}, u32[]{:S(2)}) copy-start(bf16[384,768]{1,0:T(8,128)(2,1)} %copy-done.2) | copy-start | bytes 1769476
  131.9 1.6 collective-permute-start.21
  134.8 25.1 %copy-start.14 = (f32[6]{0:T(128)S(1)}, f32[6]{0:T(128)}, u32[]{:S(2)}) copy-start(f32[6]{0:T(128)} %param.25) | copy-start | bytes 76
  134.8 12.9 %all-to-all-start.1 = ((bf16[16,8,768]{2,1,0:T(8,128)(2,1)}), bf16[16,8,768]{2,1,0:T(8,128)(2,1)S(1)}, u32[]{:S(2)}, u32[]{:S(2)}) async-start(bf16[16,8,768]{2,1,0:T(8,128)(2,1)} %shard_map.141), calls=%async_computation.1 | async-start | bytes 393216 | tf_op jit(solution)/shard_map/all_to_all | solution.py:328

commit v2 on v1

v2 whole, which is shorter than its diff:
```python
import jax
import jax.numpy as jnp
from jax import lax
from jax.experimental import pallas as pl
from jax.experimental.pallas import tpu as pltpu
from jax.sharding import Mesh, PartitionSpec as P


AXES = ("x", "y", "z", "core")
DEVICES = [(x, y, z, c) for x in range(4) for y in range(4) for z in range(4) for c in range(2)]
F32 = jnp.float32
BF16 = jnp.bfloat16
NT = (((1,), (1,)), ((), ()))


def device_id(x, y, z, c):
    return x * 32 + y * 8 + z * 2 + c


def shift_pairs(axis, step):
    pairs = []
    for place in DEVICES:
        goal = list(place)
        goal[axis] = (goal[axis] + (step if place[3] == 0 else -step)) % 4
        pairs.append((device_id(*place), device_id(*goal)))
    return pairs


SWAP = [(i, i ^ 1) for i in range(128)]


def swapped(array):
    return lax.ppermute(array, AXES, SWAP)


def ring(array, axis, direct=False):
    ahead = lax.ppermute(array, AXES, shift_pairs(axis, 1))
    behind = lax.ppermute(array, AXES, shift_pairs(axis, -1))
    if direct:
        far = lax.ppermute(array, AXES, shift_pairs(axis, 2))
    else:
        far = lax.ppermute(ahead, AXES, shift_pairs(axis, 1))
    return [array, ahead, behind, far]


def call(body, outs, args, grid=(1,), ins=None, out_specs=None, scratch=(), prefetch=0, limit=16):
    whole = lambda s: pl.BlockSpec(s, lambda *_: (0,) * len(s))
    ins = ins or [None] * (len(args) - prefetch)
    ins = [b or whole(a.shape) for b, a in zip(ins, args[prefetch:])]
    out_specs = out_specs or [whole(o.shape) for o in outs]
    return pl.pallas_call(
        body,
        out_shape=outs,
        grid_spec=pltpu.PrefetchScalarGridSpec(
            num_scalar_prefetch=prefetch, grid=grid, in_specs=ins, out_specs=out_specs, scratch_shapes=list(scratch)
        ),
        compiler_params=pltpu.CompilerParams(vmem_limit_bytes=limit << 20),
    )(*args)


def norm_rows(values, gain):
    centre = values - jnp.mean(values, axis=-1, keepdims=True)
    spread = jnp.mean(centre * centre, axis=-1, keepdims=True)
    return centre * lax.rsqrt(spread + 1e-06) * gain


def nearby():
    sign = 1 - 2 * lax.axis_index("core")
    offsets = (0, -sign, sign, 2)
    return [[(lax.axis_index(axis) + offset) & 3 for offset in offsets] for axis in AXES[:3]]


def split(values):
    high = values.astype(BF16)
    return high, (values - high.astype(F32)).astype(BF16)


def block_ones(size, block):
    row = lax.broadcasted_iota(jnp.int32, (size, size), 0) // block
    col = lax.broadcasted_iota(jnp.int32, (size, size), 1) // block
    return (row == col).astype(F32).astype(BF16)


def norm_kernel(own, other, gain, own_out, other_out):
    own_out[...] = norm_rows(own[...].astype(F32), gain[...]).astype(BF16)
    other_out[...] = norm_rows(other[...].astype(F32), gain[...]).astype(BF16)


def unpack_kernel(m0, m1, m2, m3, ups, downs):
    for r, m in enumerate((m0, m1, m2, m3)):
        ups[r * 64 : (r + 1) * 64] = m[0:64]
        downs[r * 64 : (r + 1) * 64] = m[64:128]


def join_kernel(a, b, c, d, out):
    size = a.shape[0]
    for r, part in enumerate((a, b, c, d)):
        out[r * size : (r + 1) * size] = part[...]


def interleave_kernel(a, b, c, d, out):
    for r, part in enumerate((a, b, c, d)):
        for k in range(4):
            out[(k * 4 + r) * 64 : (k * 4 + r + 1) * 64] = part[k * 64 : (k + 1) * 64]


def settle_kernel(scale, a, b, c, d, out):
    xs, ys, _ = nearby()
    for r, part in enumerate((a, b, c, d)):
        for k in range(4):
            at = pl.multiple_of((xs[k] * 4 + ys[r]) * 64, 64)
            out[pl.ds(at, 64), :] = part[k * 64 : (k + 1) * 64]
    lane = lax.broadcasted_iota(jnp.int32, (16, 512), 1)
    row = lax.broadcasted_iota(jnp.int32, (16, 512), 0)
    value = jnp.where(lane < 64, scale[0], scale[1])
    high = value.astype(BF16).astype(F32)
    middle = (value - high).astype(BF16).astype(F32)
    low = value - high - middle
    out[1024:1040] = jnp.where(
        row == 0, high, jnp.where(row == 1, middle, jnp.where(row == 2, low, 0.0))
    ).astype(BF16)


def attend_kernel(own, other, piece, out):
    scale = jnp.sum(piece[1024:1040, 0:128].astype(F32), axis=0, keepdims=True)
    ones = block_ones(256, 64)
    lane = lax.broadcasted_iota(jnp.int32, (64, 128), 1)
    first = lane < 64
    nil = jnp.zeros((64, 128), F32)
    for side, rows in enumerate((own, other)):
        joint = jnp.dot(rows[...], piece[0:1024, 0:384], preferred_element_type=F32)
        pair = joint[:, 0:256]
        high, low = split(pair * pair)
        squares = jnp.dot(high, ones, preferred_element_type=F32) + jnp.dot(low, ones, preferred_element_type=F32)
        unit = pair * lax.rsqrt(squares + 1e-06)
        for i in range(6):
            at = slice(i * 64, (i + 1) * 64)
            query = unit[at, 0:128].astype(BF16)
            key = unit[at, 128:256]
            value = joint[at, 256:384]
            keys = jnp.concatenate([jnp.where(first, key, nil), jnp.where(first, nil, key)], axis=0).astype(BF16)
            values = jnp.concatenate([jnp.where(first, value, nil), jnp.where(first, nil, value)], axis=0).astype(BF16)
            scores = lax.dot_general(query, keys, NT, preferred_element_type=F32)
            weights = jnp.exp(scores * scale).astype(BF16)
            mixed = jnp.dot(weights, values, preferred_element_type=F32)
            total = jnp.dot(weights, ones[0:128, 0:128], preferred_element_type=F32)
            out[side * 384 + i * 64 : side * 384 + (i + 1) * 64, :] = (mixed / total).astype(BF16)


def output_kernel(h0, h1, h2, h3, p0, p1, p2, p3, own, other):
    heads = jnp.concatenate([h0[...], h1[...], h2[...], h3[...]], axis=1)
    weight = jnp.concatenate([p0[...], p1[...], p2[...], p3[...]], axis=1)
    own[...] = lax.dot_general(heads[0:384], weight, NT, preferred_element_type=F32)
    other[...] = lax.dot_general(heads[384:768], weight, NT, preferred_element_type=F32).astype(BF16)


def residual_kernel(patches, own, other, gain, normed, pooled):
    residual = patches[...].astype(F32) + own[...] + other[...].astype(F32)
    normed[...] = norm_rows(residual, gain[...]).astype(BF16)
    pooled[0:6] = jnp.sum(residual.reshape(6, 64, 1024), axis=1) * (1.0 / 64)
    pooled[6:8] = jnp.zeros((2, 1024), F32)


def up_kernel(own, other, p0, p1, p2, p3, mean, weight):
    xs, ys, _ = nearby()
    for r, piece in enumerate((p0, p1, p2, p3)):
        for j in range(4):
            at = pl.multiple_of((xs[j] * 4 + ys[r]) * 64, 64)
            weight[pl.ds(at, 64), :] = piece[j * 64 : (j + 1) * 64, :]
    for side, rows in enumerate((own, other)):
        upper = jnp.dot(rows[...], weight[...], preferred_element_type=F32)
        hidden = (0.5 * upper * (1.0 + lax.erf(upper * 0.7071067811865476))).astype(BF16).astype(F32)
        mean[side * 8 : side * 8 + 6, :] = jnp.sum(hidden.reshape(6, 64, 512), axis=1) * (1.0 / 64)
        mean[side * 8 + 6 : side * 8 + 8, :] = jnp.zeros((2, 512), F32)


def down_kernel(mean, p0, p1, p2, p3, own, other):
    xs, ys, _ = nearby()
    high, low = split(mean[...])
    both = jnp.concatenate([high, low], axis=0)
    for r, piece in enumerate((p0, p1, p2, p3)):
        product = jnp.zeros((32, 256), F32)
        for k in range(4):
            product = product + lax.dot_general(
                both[:, k * 512 : (k + 1) * 512],
                piece[k * 256 : (k + 1) * 256, :],
                NT,
                preferred_element_type=F32,
            )
        product = product[0:16] + product[16:32]
        for j in range(4):
            own[xs[r] * 4 + ys[j]] = product[0:8, j * 64 : (j + 1) * 64]
            other[xs[r] * 4 + ys[j]] = product[8:16, j * 64 : (j + 1) * 64]


def final_kernel(pooled, own, other, gain, project, units):
    feed = jnp.concatenate([own[d] + other[d] for d in range(16)], axis=1)
    normed = norm_rows(pooled[...] + feed, gain[...]).astype(BF16)
    embedded = jnp.dot(normed, project[...], preferred_element_type=F32)
    unit = (embedded * lax.rsqrt(jnp.sum(embedded * embedded, axis=-1, keepdims=True) + 1e-06)).astype(BF16)
    for d in range(16):
        units[d] = unit


def logits_kernel(captions, units, texts, texts_other, out):
    image = units[...]
    core = lax.axis_index("core")
    xs = nearby()[0]
    place = lax.axis_index("y") * 8 + lax.axis_index("z") * 2
    column = lax.broadcasted_iota(jnp.int32, (1, 384), 1)
    logits, ids = [], []
    for rows, order, side in ((texts, (0, 1, 2, 3), core), (texts_other, (0, 2, 1, 3), 1 - core)):
        logits.append(lax.dot_general(image, rows[...], NT, preferred_element_type=F32))
        spot = column
        for block, r in enumerate(order):
            holder = (xs[r] * 32 + place + side) * 96 - block * 96
            inside = (column >= block * 96) & (column < block * 96 + 96)
            spot = jnp.where(inside, column + holder, spot)
        ids.append(spot)
    logits, ids = jnp.concatenate(logits, axis=1), jnp.concatenate(ids, axis=1)
    row = lax.broadcasted_iota(jnp.int32, (8, 1), 0)
    wanted = []
    for d in range(16):
        part = jnp.full((8, 1), -1, jnp.int32)
        for k in range(6):
            part = jnp.where(row == k, captions[(lax.axis_index("x") * 32 + d * 2 + core) * 6 + k], part)
        wanted.append(part)
    wanted = jnp.concatenate(wanted, axis=0)
    highest = jnp.max(logits, axis=1, keepdims=True)
    total = jnp.sum(jnp.exp(logits - highest), axis=1, keepdims=True)
    matched = jnp.sum(jnp.where(wanted == ids, logits, 0.0), axis=1, keepdims=True)
    lane = lax.broadcasted_iota(jnp.int32, (128, 128), 1)
    out[...] = jnp.where(lane == 0, highest, jnp.where(lane == 1, total, matched))


def loss_kernel(parts, baseline, loss):
    highest = parts[0]
    for i in range(1, 16):
        highest = jnp.maximum(highest, parts[i])
    highest = highest[:, 0:1]
    total = jnp.zeros((8, 1), F32)
    matched = jnp.zeros((8, 1), F32)
    for i in range(16):
        part = parts[i]
        total = total + part[:, 1:2] * jnp.exp(part[:, 0:1] - highest)
        matched = matched + part[:, 2:3]
    value = highest + jnp.log(total) - matched
    row = lax.broadcasted_iota(jnp.int32, (8, 128), 0)
    lane = lax.broadcasted_iota(jnp.int32, (8, 128), 1)
    across = jnp.sum(jnp.where(row == lane, value, 0.0), axis=0)
    loss[...] = across[0:6] - baseline[...]


def shards(
    patches,
    gain_first,
    joint_weight,
    head_scale,
    output_weight,
    gain_second,
    up_weight,
    down_weight,
    gain_final,
    project_weight,
    text_bank,
    captions,
    reference_loss,
):
    rows = patches.reshape(384, 1024)
    rows_other = swapped(rows)
    sds = jax.ShapeDtypeStruct

    front = jnp.concatenate([joint_weight[:, part] for part in range(3)] + [output_weight.T], axis=1)
    message = jnp.concatenate([up_weight, down_weight.T], axis=0)
    small = dict(limit=6)
    first_a = call(join_kernel, [sds((256, 512), BF16)], ring(front, 0, direct=True), **small)[0]
    second_a = call(settle_kernel, [sds((1040, 512), BF16)], [head_scale, *ring(first_a, 1)], prefetch=1, **small)[0]
    pieces_a = ring(second_a, 2)
    messages = ring(message, 2)
    first_b, first_c = call(unpack_kernel, [sds((256, 512), BF16), sds((256, 512), BF16)], messages, limit=4)
    texts_own = call(join_kernel, [sds((384, 768), BF16)], ring(text_bank, 0), **small)[0]
    second_b = call(interleave_kernel, [sds((1024, 512), BF16)], ring(first_b, 0), limit=6)[0]
    second_c = call(interleave_kernel, [sds((1024, 512), BF16)], ring(first_c, 1), limit=6)[0]
    pieces_b = ring(second_b, 1)
    pieces_c = ring(second_c, 0)
    texts_other = swapped(texts_own)

    gain_row = gain_first.reshape(1, 1024)
    normed_own, normed_other = call(norm_kernel, [sds((384, 1024), BF16)] * 2, [rows, rows_other, gain_row], limit=8)
    heads = []
    for piece in pieces_a:
        heads += call(attend_kernel, [sds((768, 128), BF16)], [normed_own, normed_other, piece], limit=10)
    last = pl.BlockSpec((1024, 128), lambda *_: (0, 3))
    part_own, part_other = call(
        output_kernel, [sds((384, 1024), F32), sds((384, 1024), BF16)], [*heads, *pieces_a], ins=[None] * 4 + [last] * 4
    )
    normed_two, pooled = call(
        residual_kernel,
        [sds((384, 1024), BF16), sds((8, 1024), F32)],
        [rows, part_own, swapped(part_other), gain_second.reshape(1, 1024)],
        limit=12,
    )
    quarter = pl.BlockSpec((256, 512), lambda i, *_: (i, 0))
    mean = call(
        up_kernel,
        [sds((16, 2048), F32)],
        [normed_two, swapped(normed_two), *pieces_b],
        grid=(4,),
        ins=[None] * 2 + [quarter] * 4,
        out_specs=[pl.BlockSpec((16, 512), lambda i, *_: (0, i))],
        scratch=[pltpu.VMEM((1024, 512), BF16)],
    )[0]
    feed_own, feed_other = call(down_kernel, [sds((16, 8, 64), F32)] * 2, [mean, *pieces_c], limit=24)
    units = call(
        final_kernel,
        [sds((16, 8, 768), BF16)],
        [pooled, feed_own, swapped(feed_other), gain_final.reshape(1, 1024), project_weight],
    )[0]

    everyone = lax.all_to_all(units, ("y", "z"), 0, 0, tiled=True)
    parts = call(
        logits_kernel,
        [sds((128, 128), F32)],
        [captions, everyone.reshape(128, 768), texts_own, texts_other],
        prefetch=1,
    )[0]
    parts = lax.all_to_all(parts.reshape(16, 8, 128), ("y", "z"), 0, 0, tiled=True)
    return call(loss_kernel, [sds((6,), F32)], [parts, reference_loss])[0]


def solution(mesh):
    grid = Mesh(mesh.devices.reshape(4, 4, 4, 2), AXES)
    dp, mp = ("x", "y"), ("z", "core")
    placed = (
        P(AXES, None, None),
        P(),
        P(dp, None, mp),
        P(mp),
        P(mp, dp),
        P(),
        P(dp, mp),
        P(mp, dp),
        P(),
        P(),
        P(AXES, None),
        P(),
        P(AXES),
    )

    return jax.shard_map(shards, mesh=grid, in_specs=placed, out_specs=P(AXES), check_vma=False)
```

time: 162 us -> 170 us (1.049)
  blocking collectives: 33.6 us -> 9.94 us
  waiting for transfers between devices: 48.4 us -> 70.3 us
  starting transfers between devices: 45.1 us -> 61.5 us
  Pallas kernels: 29.3 us -> 23.8 us
    all_to_all x2 -> x1, blocking collectives: 33.6 us -> 9.94 us  [shards(): lax.all_to_all(parts.reshape(16, 8, 128), ('y', 'z'), 0, 0, tiled=True)]
    ppermute x6 -> x8, waiting for transfers between devices: 4.46 us -> 27.4 us  [ring(): far = lax.ppermute(ahead, AXES, shift_pairs(axis, 1))]
    ppermute x6 -> x9, starting transfers between devices: 9.87 us -> 23.7 us  [ring(): ahead = lax.ppermute(array, AXES, shift_pairs(axis, 1))]
    ppermute x6 -> x9, waiting for transfers between devices: 20.8 us -> 14.6 us  [ring(): behind = lax.ppermute(array, AXES, shift_pairs(axis, -1))]
    pallas_call x17 -> x18, Pallas kernels: 29.3 us -> 23.8 us  [call(): pl.pallas_call(body, out_shape=outs, grid_spec=pltpu.PrefetchScalarGridSp...]
    ppermute x6 -> x8, starting transfers between devices: 15.9 us -> 20.9 us  [ring(): far = lax.ppermute(ahead, AXES, shift_pairs(axis, 1))]
    ppermute x5, starting transfers between devices: 11.1 us -> 7.62 us  [swapped(): return lax.ppermute(array, AXES, SWAP)]
    ppermute x6 -> x9, waiting for transfers between devices: 15.7 us -> 18.6 us  [ring(): ahead = lax.ppermute(array, AXES, shift_pairs(axis, 1))]
  transfers between devices with their start and end apart: 24 -> 33, of which waited for: 7 -> 15; matrix products, arithmetic and copies ran while one was open for 0% -> 0% of each run, Pallas kernels for 17% -> 13%
where the time goes in v2:
time: 170 us; the launch traced here: 168 us
  waiting for transfers between devices  70.3 us (41%)
  starting transfers between devices  61.5 us (36%)
  Pallas kernels  23.8 us (14%)
  blocking collectives  9.94 us (6%)
    ppermute x8, waiting for transfers between devices, ring(): far = lax.ppermute(ahead, AXES, shift_pairs(axis, 1))  27.4 us
    pallas_call x18, Pallas kernels, call(): pl.pallas_call(body, out_shape=outs, grid_spec=pltpu.PrefetchScalarGridSp...  23.8 us
    ppermute x9, starting transfers between devices, ring(): ahead = lax.ppermute(array, AXES, shift_pairs(axis, 1))  23.7 us
    ppermute x8, starting transfers between devices, ring(): far = lax.ppermute(ahead, AXES, shift_pairs(axis, 1))  20.9 us
    ppermute x9, waiting for transfers between devices, ring(): ahead = lax.ppermute(array, AXES, shift_pairs(axis, 1))  18.6 us
    ppermute x9, waiting for transfers between devices, ring(): behind = lax.ppermute(array, AXES, shift_pairs(axis, -1))  14.6 us
    all_to_all x1, blocking collectives, shards(): lax.all_to_all(parts.reshape(16, 8, 128), ('y', 'z'), 0, 0, tiled=True)  9.94 us
    ppermute x5, starting transfers between devices, swapped(): return lax.ppermute(array, AXES, SWAP)  7.62 us
  transfers between devices with their start and end apart: 33, of which 15 were waited for; matrix products, arithmetic and copies ran while one was open for 0% of the time, Pallas kernels for 13%

profile of v2, /device:TPU:1, one launch (start us, length us, event | category | flops | bytes accessed | tf_op | source)
XLA Modules:
  0.0 168.1 jit_solution(17651397148635289850)
XLA Ops:
  0.0 0.8 slice_bitcast_fusion.2
  1.5 3.4 %collective-permute-start.1 = (bf16[64,512]{1,0:T(8,128)(2,1)S(1)}, bf16[64,512]{1,0:T(8,128)(2,1)S(1)}, u32[]{:S(2)}, u32[]{:S(2)}) collective-permute-start(bf16[64,512]{1,0:T(8,128)(2,1)S(1)} %pad_maximum_fusion.1.a), channel_id=1, source_target_pairs={{0,32},{1,97},{2,34},{3,99},{4,36},{5,101},{6,38},{7,103},{8,40},{... | collective-permute-start | bytes 196616 | tf_op jit(solution)/shard_map/ppermute | solution.py:37
  4.9 1.7 %collective-permute-start.3 = (bf16[64,512]{1,0:T(8,128)(2,1)S(1)}, bf16[64,512]{1,0:T(8,128)(2,1)S(1)}, u32[]{:S(2)}, u32[]{:S(2)}) collective-permute-start(bf16[64,512]{1,0:T(8,128)(2,1)S(1)} %pad_maximum_fusion.1.a), channel_id=1, source_target_pairs={{0,64},{1,65},{2,66},{3,67},{4,68},{5,69},{6,70},{7,71},{8,72},{9,... | collective-permute-start | bytes 196616 | tf_op jit(solution)/shard_map/ppermute | solution.py:40
  6.6 3.3 %collective-permute-done.2.c = bf16[64,512]{1,0:T(8,128)(2,1)S(1)} collective-permute-done((bf16[64,512]{1,0:T(8,128)(2,1)S(1)}, bf16[64,512]{1,0:T(8,128)(2,1)S(1)}, u32[]{:S(2)}, u32[]{:S(2)}) %collective-permute-start.2) | collective-permute-done | bytes 65568 | tf_op jit(solution)/shard_map/ppermute | solution.py:38
  9.9 2.8 %collective-permute-start.4 = (bf16[256,512]{1,0:T(8,128)(2,1)S(1)}, bf16[256,512]{1,0:T(8,128)(2,1)S(1)}, u32[]{:S(2)}, u32[]{:S(2)}) collective-permute-start(bf16[256,512]{1,0:T(8,128)(2,1)S(1)} %shard_map.128.a), channel_id=1, source_target_pairs={{0,8},{1,25},{2,10},{3,27},{4,12},{5,29},{6,14},{7,31},{8,16},{9,1... | collective-permute-start | bytes 786440 | tf_op jit(solution)/shard_map/ppermute | solution.py:37
  12.7 3.3 %collective-permute-done.4.b = bf16[256,512]{1,0:T(8,128)(2,1)S(1)} collective-permute-done((bf16[256,512]{1,0:T(8,128)(2,1)S(1)}, bf16[256,512]{1,0:T(8,128)(2,1)S(1)}, u32[]{:S(2)}, u32[]{:S(2)}) %collective-permute-start.4) | collective-permute-done | bytes 262176 | tf_op jit(solution)/shard_map/ppermute | solution.py:37
  16.0 3.5 %collective-permute-start.6 = (bf16[256,512]{1,0:T(8,128)(2,1)S(1)}, bf16[256,512]{1,0:T(8,128)(2,1)S(1)}, u32[]{:S(2)}, u32[]{:S(2)}) collective-permute-start(bf16[256,512]{1,0:T(8,128)(2,1)S(1)} %collective-permute-done.4.b), channel_id=1, source_target_pairs={{0,8},{1,25},{2,10},{3,27},{4,12},{5,29},{6,14},{7,31},{8,16},{9,1... | collective-permute-start | bytes 786440 | tf_op jit(solution)/shard_map/ppermute | solution.py:42
  19.5 2.3 %collective-permute-done.5.c = bf16[256,512]{1,0:T(8,128)(2,1)S(1)} collective-permute-done((bf16[256,512]{1,0:T(8,128)(2,1)S(1)}, bf16[256,512]{1,0:T(8,128)(2,1)S(1)}, u32[]{:S(2)}, u32[]{:S(2)}) %collective-permute-start.5) | collective-permute-done | bytes 262176 | tf_op jit(solution)/shard_map/ppermute | solution.py:38
  21.8 1.0 collective-permute-done.6.d
  24.1 3.5 %collective-permute-start.7 = (bf16[1040,512]{1,0:T(8,128)(2,1)S(1)}, bf16[1040,512]{1,0:T(8,128)(2,1)S(1)}, u32[]{:S(2)}, u32[]{:S(2)}) collective-permute-start(bf16[1040,512]{1,0:T(8,128)(2,1)S(1)} %shard_map.129.piece.p0), channel_id=1, source_target_pairs={{0,2},{1,7},{2,4},{3,1},{4,6},{5,3},{6,0},{7,5},{8,10},{9,15},{10,... | collective-permute-start | bytes 3194888 | tf_op jit(solution)/shard_map/ppermute | solution.py:37
  27.8 1.3 collective-permute-start.13
  29.1 13.2 %collective-permute-done.12.m1 = bf16[128,512]{1,0:T(8,128)(2,1)S(1)} collective-permute-done((bf16[128,512]{1,0:T(8,128)(2,1)S(1)}, bf16[128,512]{1,0:T(8,128)(2,1)S(1)}, u32[]{:S(2)}, u32[]{:S(2)}) %collective-permute-start.12) | collective-permute-done | bytes 131104 | tf_op jit(solution)/shard_map/ppermute | solution.py:37
  42.3 3.1 %collective-permute-start.14 = (bf16[128,512]{1,0:T(8,128)(2,1)S(1)}, bf16[128,512]{1,0:T(8,128)(2,1)S(1)}, u32[]{:S(2)}, u32[]{:S(2)}) collective-permute-start(bf16[128,512]{1,0:T(8,128)(2,1)S(1)} %collective-permute-done.12.m1), channel_id=1, source_target_pairs={{0,2},{1,7},{2,4},{3,1},{4,6},{5,3},{6,0},{7,5},{8,10},{9,15},{10,... | collective-permute-start | bytes 393224 | tf_op jit(solution)/shard_map/ppermute | solution.py:42
  45.4 1.9 %collective-permute-done.14.m3 = bf16[128,512]{1,0:T(8,128)(2,1)S(1)} collective-permute-done((bf16[128,512]{1,0:T(8,128)(2,1)S(1)}, bf16[128,512]{1,0:T(8,128)(2,1)S(1)}, u32[]{:S(2)}, u32[]{:S(2)}) %collective-permute-start.14) | collective-permute-done | bytes 131104 | tf_op jit(solution)/shard_map/ppermute | solution.py:42
  47.4 4.4 %collective-permute-start.15 = (bf16[256,512]{1,0:T(8,128)(2,1)S(1)}, bf16[256,512]{1,0:T(8,128)(2,1)S(1)}, u32[]{:S(2)}, u32[]{:S(2)}) collective-permute-start(bf16[256,512]{1,0:T(8,128)(2,1)S(1)} %get-tuple-element.21.a), channel_id=1, source_target_pairs={{0,32},{1,97},{2,34},{3,99},{4,36},{5,101},{6,38},{7,103},{8,40},{... | collective-permute-start | bytes 786440 | tf_op jit(solution)/shard_map/ppermute | solution.py:37
  51.8 3.1 %collective-permute-start.9 = (bf16[1040,512]{1,0:T(8,128)(2,1)S(1)}, bf16[1040,512]{1,0:T(8,128)(2,1)S(1)}, u32[]{:S(2)}, u32[]{:S(2)}) collective-permute-start(bf16[1040,512]{1,0:T(8,128)(2,1)S(1)} %collective-permute-done.7.piece.p1), channel_id=1, source_target_pairs={{0,2},{1,7},{2,4},{3,1},{4,6},{5,3},{6,0},{7,5},{8,10},{9,15},{10,... | collective-permute-start | bytes 3194888 | tf_op jit(solution)/shard_map/ppermute | solution.py:42
  54.9 3.1 %collective-permute-start.21 = (bf16[256,512]{1,0:T(8,128)(2,1)S(1)}, bf16[256,512]{1,0:T(8,128)(2,1)S(1)}, u32[]{:S(2)}, u32[]{:S(2)}) collective-permute-start(bf16[256,512]{1,0:T(8,128)(2,1)S(1)} %get-tuple-element.22.a), channel_id=1, source_target_pairs={{0,8},{1,25},{2,10},{3,27},{4,12},{5,29},{6,14},{7,31},{8,16},{9,1... | collective-permute-start | bytes 786440 | tf_op jit(solution)/shard_map/ppermute | solution.py:37
  58.0 2.7 %collective-permute-start.17 = (bf16[256,512]{1,0:T(8,128)(2,1)S(1)}, bf16[256,512]{1,0:T(8,128)(2,1)S(1)}, u32[]{:S(2)}, u32[]{:S(2)}) collective-permute-start(bf16[256,512]{1,0:T(8,128)(2,1)S(1)} %collective-permute-done.15.b), channel_id=1, source_target_pairs={{0,32},{1,97},{2,34},{3,99},{4,36},{5,101},{6,38},{7,103},{8,40},{... | collective-permute-start | bytes 786440 | tf_op jit(solution)/shard_map/ppermute | solution.py:42
  60.7 2.1 %collective-permute-done.16.c = bf16[256,512]{1,0:T(8,128)(2,1)S(1)} collective-permute-done((bf16[256,512]{1,0:T(8,128)(2,1)S(1)}, bf16[256,512]{1,0:T(8,128)(2,1)S(1)}, u32[]{:S(2)}, u32[]{:S(2)}) %collective-permute-start.16) | collective-permute-done | bytes 262176 | tf_op jit(solution)/shard_map/ppermute | solution.py:38
  62.8 4.4 %collective-permute-start = (bf16[384,1024]{1,0:T(8,128)(2,1)S(1)}, bf16[384,1024]{1,0:T(8,128)(2,1)S(1)}, u32[]{:S(2)}, u32[]{:S(2)}) collective-permute-start(bf16[384,1024]{1,0:T(8,128)(2,1)S(1)} %bitcast.14), channel_id=1, source_target_pairs={{0,1},{1,0},{2,3},{3,2},{4,5},{5,4},{6,7},{7,6},{8,9},{9,8},{10,11... | collective-permute-start | bytes 2359304 | tf_op jit(solution)/shard_map/ppermute | solution.py:33
  67.2 2.7 %collective-permute-start.23 = (bf16[256,512]{1,0:T(8,128)(2,1)S(1)}, bf16[256,512]{1,0:T(8,128)(2,1)S(1)}, u32[]{:S(2)}, u32[]{:S(2)}) collective-permute-start(bf16[256,512]{1,0:T(8,128)(2,1)S(1)} %collective-permute-done.21.b), channel_id=1, source_target_pairs={{0,8},{1,25},{2,10},{3,27},{4,12},{5,29},{6,14},{7,31},{8,16},{9,1... | collective-permute-start | bytes 786440 | tf_op jit(solution)/shard_map/ppermute | solution.py:42
  70.0 4.0 %collective-permute-done.22.c = bf16[256,512]{1,0:T(8,128)(2,1)S(1)} collective-permute-done((bf16[256,512]{1,0:T(8,128)(2,1)S(1)}, bf16[256,512]{1,0:T(8,128)(2,1)S(1)}, u32[]{:S(2)}, u32[]{:S(2)}) %collective-permute-start.22) | collective-permute-done | bytes 262176 | tf_op jit(solution)/shard_map/ppermute | solution.py:38
  73.9 1.3 collective-permute-done.23.d
  75.3 3.7 %collective-permute-start.24 = (bf16[1024,512]{1,0:T(8,128)(2,1)S(1)}, bf16[1024,512]{1,0:T(8,128)(2,1)S(1)}, u32[]{:S(2)}, u32[]{:S(2)}) collective-permute-start(bf16[1024,512]{1,0:T(8,128)(2,1)S(1)} %shard_map.139.p0), channel_id=1, source_target_pairs={{0,32},{1,97},{2,34},{3,99},{4,36},{5,101},{6,38},{7,103},{8,40},{... | collective-permute-start | bytes 3145736 | tf_op jit(solution)/shard_map/ppermute | solution.py:37
  79.0 1.0 shard_map.127
  80.0 2.5 %shard_map.130.h0 = bf16[768,128]{1,0:T(8,128)(2,1)S(1)} custom-call(bf16[384,1024]{1,0:T(8,128)(2,1)S(1)} %get-tuple-element.15.own, bf16[384,1024]{1,0:T(8,128)(2,1)S(1)} %get-tuple-element.16.other, bf16[1040,512]{1,0:T(8,128)(2,1)S(1)} %shard_map.129.piece.p0), custom_call_target="tpu_custom_call" | custom-call | tf_op jit(solution)/shard_map/pallas_call | solution.py:51
  82.5 2.5 %shard_map.131.h1 = bf16[768,128]{1,0:T(8,128)(2,1)S(1)} custom-call(bf16[384,1024]{1,0:T(8,128)(2,1)S(1)} %get-tuple-element.15.own, bf16[384,1024]{1,0:T(8,128)(2,1)S(1)} %get-tuple-element.16.other, bf16[1040,512]{1,0:T(8,128)(2,1)S(1)} %collective-permute-done.7.piece.p1), custom_call_target="tpu_custom_call" | custom-call | tf_op jit(solution)/shard_map/pallas_call | solution.py:51
  85.1 2.5 %shard_map.132.h2 = bf16[768,128]{1,0:T(8,128)(2,1)S(1)} custom-call(bf16[384,1024]{1,0:T(8,128)(2,1)S(1)} %get-tuple-element.15.own, bf16[384,1024]{1,0:T(8,128)(2,1)S(1)} %get-tuple-element.16.other, bf16[1040,512]{1,0:T(8,128)(2,1)S(1)} %collective-permute-done.8.piece.p2), custom_call_target="tpu_custom_call" | custom-call | tf_op jit(solution)/shard_map/pallas_call | solution.py:51
  87.6 2.5 %shard_map.133.h3 = bf16[768,128]{1,0:T(8,128)(2,1)S(1)} custom-call(bf16[384,1024]{1,0:T(8,128)(2,1)S(1)} %get-tuple-element.15.own, bf16[384,1024]{1,0:T(8,128)(2,1)S(1)} %get-tuple-element.16.other, bf16[1040,512]{1,0:T(8,128)(2,1)S(1)} %collective-permute-done.9.piece.p3), custom_call_target="tpu_custom_call" | custom-call | tf_op jit(solution)/shard_map/pallas_call | solution.py:51
  90.2 1.1 shard_map.134
  91.2 1.4 collective-permute-start.10
  92.9 2.7 %collective-permute-start.28 = (bf16[96,768]{1,0:T(8,128)(2,1)S(1)}, bf16[96,768]{1,0:T(8,128)(2,1)S(1)}, u32[]{:S(2)}, u32[]{:S(2)}) collective-permute-start(bf16[96,768]{1,0:T(8,128)(2,1)S(1)} %copy-done.2), channel_id=1, source_target_pairs={{0,32},{1,97},{2,34},{3,99},{4,36},{5,101},{6,38},{7,103},{8,40},{... | collective-permute-start | bytes 442376 | tf_op jit(solution)/shard_map/ppermute | solution.py:37
  95.6 2.1 %collective-permute-done.28.b = bf16[96,768]{1,0:T(8,128)(2,1)S(1)} collective-permute-done((bf16[96,768]{1,0:T(8,128)(2,1)S(1)}, bf16[96,768]{1,0:T(8,128)(2,1)S(1)}, u32[]{:S(2)}, u32[]{:S(2)}) %collective-permute-start.28) | collective-permute-done | bytes 147488 | tf_op jit(solution)/shard_map/ppermute | solution.py:37
  97.7 2.7 %collective-permute-start.20 = (bf16[1024,512]{1,0:T(8,128)(2,1)S(1)}, bf16[1024,512]{1,0:T(8,128)(2,1)S(1)}, u32[]{:S(2)}, u32[]{:S(2)}) collective-permute-start(bf16[1024,512]{1,0:T(8,128)(2,1)S(1)} %collective-permute-done.18.p1), channel_id=1, source_target_pairs={{0,8},{1,25},{2,10},{3,27},{4,12},{5,29},{6,14},{7,31},{8,16},{9,1... | collective-permute-start | bytes 3145736 | tf_op jit(solution)/shard_map/ppermute | solution.py:42
  100.4 3.0 %collective-permute-done.29.c = bf16[96,768]{1,0:T(8,128)(2,1)S(1)} collective-permute-done((bf16[96,768]{1,0:T(8,128)(2,1)S(1)}, bf16[96,768]{1,0:T(8,128)(2,1)S(1)}, u32[]{:S(2)}, u32[]{:S(2)}) %collective-permute-start.29) | collective-permute-done | bytes 147488 | tf_op jit(solution)/shard_map/ppermute | solution.py:38
  103.4 2.7 %collective-permute-start.26 = (bf16[1024,512]{1,0:T(8,128)(2,1)S(1)}, bf16[1024,512]{1,0:T(8,128)(2,1)S(1)}, u32[]{:S(2)}, u32[]{:S(2)}) collective-permute-start(bf16[1024,512]{1,0:T(8,128)(2,1)S(1)} %collective-permute-done.24.p1), channel_id=1, source_target_pairs={{0,32},{1,97},{2,34},{3,99},{4,36},{5,101},{6,38},{7,103},{8,40},{... | collective-permute-start | bytes 3145736 | tf_op jit(solution)/shard_map/ppermute | solution.py:42
  107.3 23.2 %collective-permute-done.30.d = bf16[96,768]{1,0:T(8,128)(2,1)S(1)} collective-permute-done((bf16[96,768]{1,0:T(8,128)(2,1)S(1)}, bf16[96,768]{1,0:T(8,128)(2,1)S(1)}, u32[]{:S(2)}, u32[]{:S(2)}) %collective-permute-start.30) | collective-permute-done | bytes 147488 | tf_op jit(solution)/shard_map/ppermute | solution.py:42
  130.5 1.3 collective-permute-start.11
  131.9 1.8 %collective-permute-done.11.other = bf16[384,1024]{1,0:T(8,128)(2,1)S(1)} collective-permute-done((bf16[384,1024]{1,0:T(8,128)(2,1)S(1)}, bf16[384,1024]{1,0:T(8,128)(2,1)S(1)}, u32[]{:S(2)}, u32[]{:S(2)}) %collective-permute-start.11) | collective-permute-done | bytes 786464 | tf_op jit(solution)/shard_map/ppermute | solution.py:33
  133.6 5.4 %shard_map.138.mean = f32[16,2048]{1,0:T(8,128)S(1)} custom-call(bf16[384,1024]{1,0:T(8,128)(2,1)S(1)} %get-tuple-element.20.own, bf16[384,1024]{1,0:T(8,128)(2,1)S(1)} %collective-permute-done.11.other, bf16[1024,512]{1,0:T(8,128)(2,1)S(1)} %shard_map.137.p0, bf16[1024,512]{1,0:T(8,128)(2,1)S(1)} %collective-permute-done.18.p1, ...), custom_call_target="tpu_custom_call" | custom-call | tf_op jit(solution)/shard_map/pallas_call | solution.py:51
  139.1 1.4 shard_map.140
  140.9 0.9 collective-permute-done.27.other
  141.8 1.3 shard_map.141
  143.1 6.0 %all-to-all-start = ((bf16[16,8,768]{2,1,0:T(8,128)(2,1)}), bf16[16,8,768]{2,1,0:T(8,128)(2,1)S(1)}, u32[]{:S(2)}, u32[]{:S(2)}) async-start(bf16[16,8,768]{2,1,0:T(8,128)(2,1)} %shard_map.141), calls=%async_computation | async-start | bytes 393216 | tf_op jit(solution)/shard_map/all_to_all | solution.py:320
  149.1 7.0 %all-to-all-done = bf16[16,8,768]{2,1,0:T(8,128)(2,1)S(1)} async-done(((bf16[16,8,768]{2,1,0:T(8,128)(2,1)}), bf16[16,8,768]{2,1,0:T(8,128)(2,1)S(1)}, u32[]{:S(2)}, u32[]{:S(2)}) %all-to-all-start) | async-done | bytes 196640 | tf_op jit(solution)/shard_map/all_to_all | solution.py:320
  156.1 1.2 shard_map.143
  157.4 9.9 %all_to_all.10.parts = f32[16,8,128]{2,1,0:T(8,128)S(1)} all-to-all(f32[16,8,128]{2,1,0:T(8,128)S(1)} %bitcast.18), channel_id=1, replica_groups=mesh['x'=4,'y'=4,'z'=4,'core'=2] {'y','z'}, dimensions={0} | all-to-all | bytes 131072 | tf_op jit(solution)/shard_map/all_to_all | solution.py:327
  167.3 0.8 shard_map.144
  (62 shorter events, 4.5 us)
Async XLA Ops:
  1.5 5.1 %collective-permute-start.1 = (bf16[64,512]{1,0:T(8,128)(2,1)S(1)}, bf16[64,512]{1,0:T(8,128)(2,1)S(1)}, u32[]{:S(2)}, u32[]{:S(2)}) collective-permute-start(bf16[64,512]{1,0:T(8,128)(2,1)S(1)} %pad_maximum_fusion.1.a), channel_id=1, source_target_pairs={{0,32},{1,97},{2,34},{3,99},{4,36},{5,101},{6,38},{7,103},{8,40},{... | collective-permute-start | bytes 196616 | tf_op jit(solution)/shard_map/ppermute | solution.py:37
  4.9 5.0 %collective-permute-start.2 = (bf16[64,512]{1,0:T(8,128)(2,1)S(1)}, bf16[64,512]{1,0:T(8,128)(2,1)S(1)}, u32[]{:S(2)}, u32[]{:S(2)}) collective-permute-start(bf16[64,512]{1,0:T(8,128)(2,1)S(1)} %pad_maximum_fusion.1.a), channel_id=1, source_target_pairs={{0,96},{1,33},{2,98},{3,35},{4,100},{5,37},{6,102},{7,39},{8,104},... | collective-permute-start | bytes 196616 | tf_op jit(solution)/shard_map/ppermute | solution.py:38
  4.9 5.0 %collective-permute-start.3 = (bf16[64,512]{1,0:T(8,128)(2,1)S(1)}, bf16[64,512]{1,0:T(8,128)(2,1)S(1)}, u32[]{:S(2)}, u32[]{:S(2)}) collective-permute-start(bf16[64,512]{1,0:T(8,128)(2,1)S(1)} %pad_maximum_fusion.1.a), channel_id=1, source_target_pairs={{0,64},{1,65},{2,66},{3,67},{4,68},{5,69},{6,70},{7,71},{8,72},{9,... | collective-permute-start | bytes 196616 | tf_op jit(solution)/shard_map/ppermute | solution.py:40
  9.9 17.7 %copy-start.9 = (bf16[512,64]{0,1:T(8,128)(2,1)S(1)}, bf16[512,64]{0,1:T(8,128)(2,1)}, u32[]{:S(2)}) copy-start(bf16[512,64]{0,1:T(8,128)(2,1)} %param.20) | copy-start | bytes 196612
  9.9 17.7 %copy-start.10 = (bf16[64,512]{1,0:T(8,128)(2,1)S(1)}, bf16[64,512]{1,0:T(8,128)(2,1)}, u32[]{:S(2)}) copy-start(bf16[64,512]{1,0:T(8,128)(2,1)} %param.19) | copy-start | bytes 196612
  9.9 52.9 %copy-start = (bf16[6,64,1024]{2,1,0:T(8,128)(2,1)S(1)}, bf16[6,64,1024]{2,1,0:T(8,128)(2,1)}, u32[]{:S(2)}) copy-start(bf16[6,64,1024]{2,1,0:T(8,128)(2,1)} %param.13) | copy-start | bytes 2359300
  9.9 6.1 %collective-permute-start.4 = (bf16[256,512]{1,0:T(8,128)(2,1)S(1)}, bf16[256,512]{1,0:T(8,128)(2,1)S(1)}, u32[]{:S(2)}, u32[]{:S(2)}) collective-permute-start(bf16[256,512]{1,0:T(8,128)(2,1)S(1)} %shard_map.128.a), channel_id=1, source_target_pairs={{0,8},{1,25},{2,10},{3,27},{4,12},{5,29},{6,14},{7,31},{8,16},{9,1... | collective-permute-start | bytes 786440 | tf_op jit(solution)/shard_map/ppermute | solution.py:37
  12.7 9.1 %collective-permute-start.5 = (bf16[256,512]{1,0:T(8,128)(2,1)S(1)}, bf16[256,512]{1,0:T(8,128)(2,1)S(1)}, u32[]{:S(2)}, u32[]{:S(2)}) collective-permute-start(bf16[256,512]{1,0:T(8,128)(2,1)S(1)} %shard_map.128.a), channel_id=1, source_target_pairs={{0,24},{1,9},{2,26},{3,11},{4,28},{5,13},{6,30},{7,15},{8,0},{9,17... | collective-permute-start | bytes 786440 | tf_op jit(solution)/shard_map/ppermute | solution.py:38
  16.0 6.8 %collective-permute-start.6 = (bf16[256,512]{1,0:T(8,128)(2,1)S(1)}, bf16[256,512]{1,0:T(8,128)(2,1)S(1)}, u32[]{:S(2)}, u32[]{:S(2)}) collective-permute-start(bf16[256,512]{1,0:T(8,128)(2,1)S(1)} %collective-permute-done.4.b), channel_id=1, source_target_pairs={{0,8},{1,25},{2,10},{3,27},{4,12},{5,29},{6,14},{7,31},{8,16},{9,1... | collective-permute-start | bytes 786440 | tf_op jit(solution)/shard_map/ppermute | solution.py:42
  22.8 0.7 copy-start.7
  24.1 27.7 %collective-permute-start.7 = (bf16[1040,512]{1,0:T(8,128)(2,1)S(1)}, bf16[1040,512]{1,0:T(8,128)(2,1)S(1)}, u32[]{:S(2)}, u32[]{:S(2)}) collective-permute-start(bf16[1040,512]{1,0:T(8,128)(2,1)S(1)} %shard_map.129.piece.p0), channel_id=1, source_target_pairs={{0,2},{1,7},{2,4},{3,1},{4,6},{5,3},{6,0},{7,5},{8,10},{9,15},{10,... | collective-permute-start | bytes 3194888 | tf_op jit(solution)/shard_map/ppermute | solution.py:37
  27.6 14.7 %collective-permute-start.12 = (bf16[128,512]{1,0:T(8,128)(2,1)S(1)}, bf16[128,512]{1,0:T(8,128)(2,1)S(1)}, u32[]{:S(2)}, u32[]{:S(2)}) collective-permute-start(bf16[128,512]{1,0:T(8,128)(2,1)S(1)} %pad_maximum_fusion.m0), channel_id=1, source_target_pairs={{0,2},{1,7},{2,4},{3,1},{4,6},{5,3},{6,0},{7,5},{8,10},{9,15},{10,... | collective-permute-start | bytes 393224 | tf_op jit(solution)/shard_map/ppermute | solution.py:37
  27.8 17.6 %collective-permute-start.13 = (bf16[128,512]{1,0:T(8,128)(2,1)S(1)}, bf16[128,512]{1,0:T(8,128)(2,1)S(1)}, u32[]{:S(2)}, u32[]{:S(2)}) collective-permute-start(bf16[128,512]{1,0:T(8,128)(2,1)S(1)} %pad_maximum_fusion.m0), channel_id=1, source_target_pairs={{0,6},{1,3},{2,0},{3,5},{4,2},{5,7},{6,4},{7,1},{8,14},{9,11},{10,... | collective-permute-start | bytes 393224 | tf_op jit(solution)/shard_map/ppermute | solution.py:38
  42.3 5.1 %collective-permute-start.14 = (bf16[128,512]{1,0:T(8,128)(2,1)S(1)}, bf16[128,512]{1,0:T(8,128)(2,1)S(1)}, u32[]{:S(2)}, u32[]{:S(2)}) collective-permute-start(bf16[128,512]{1,0:T(8,128)(2,1)S(1)} %collective-permute-done.12.m1), channel_id=1, source_target_pairs={{0,2},{1,7},{2,4},{3,1},{4,6},{5,3},{6,0},{7,5},{8,10},{9,15},{10,... | collective-permute-start | bytes 393224 | tf_op jit(solution)/shard_map/ppermute | solution.py:42
  47.4 10.6 %collective-permute-start.15 = (bf16[256,512]{1,0:T(8,128)(2,1)S(1)}, bf16[256,512]{1,0:T(8,128)(2,1)S(1)}, u32[]{:S(2)}, u32[]{:S(2)}) collective-permute-start(bf16[256,512]{1,0:T(8,128)(2,1)S(1)} %get-tuple-element.21.a), channel_id=1, source_target_pairs={{0,32},{1,97},{2,34},{3,99},{4,36},{5,101},{6,38},{7,103},{8,40},{... | collective-permute-start | bytes 786440 | tf_op jit(solution)/shard_map/ppermute | solution.py:37
  51.8 33.3 %collective-permute-start.8 = (bf16[1040,512]{1,0:T(8,128)(2,1)S(1)}, bf16[1040,512]{1,0:T(8,128)(2,1)S(1)}, u32[]{:S(2)}, u32[]{:S(2)}) collective-permute-start(bf16[1040,512]{1,0:T(8,128)(2,1)S(1)} %shard_map.129.piece.p0), channel_id=1, source_target_pairs={{0,6},{1,3},{2,0},{3,5},{4,2},{5,7},{6,4},{7,1},{8,14},{9,11},{10,... | collective-permute-start | bytes 3194888 | tf_op jit(solution)/shard_map/ppermute | solution.py:38
  51.8 35.8 %collective-permute-start.9 = (bf16[1040,512]{1,0:T(8,128)(2,1)S(1)}, bf16[1040,512]{1,0:T(8,128)(2,1)S(1)}, u32[]{:S(2)}, u32[]{:S(2)}) collective-permute-start(bf16[1040,512]{1,0:T(8,128)(2,1)S(1)} %collective-permute-done.7.piece.p1), channel_id=1, source_target_pairs={{0,2},{1,7},{2,4},{3,1},{4,6},{5,3},{6,0},{7,5},{8,10},{9,15},{10,... | collective-permute-start | bytes 3194888 | tf_op jit(solution)/shard_map/ppermute | solution.py:42
  54.9 7.9 %collective-permute-start.16 = (bf16[256,512]{1,0:T(8,128)(2,1)S(1)}, bf16[256,512]{1,0:T(8,128)(2,1)S(1)}, u32[]{:S(2)}, u32[]{:S(2)}) collective-permute-start(bf16[256,512]{1,0:T(8,128)(2,1)S(1)} %get-tuple-element.21.a), channel_id=1, source_target_pairs={{0,96},{1,33},{2,98},{3,35},{4,100},{5,37},{6,102},{7,39},{8,104},... | collective-permute-start | bytes 786440 | tf_op jit(solution)/shard_map/ppermute | solution.py:38
  54.9 12.3 %collective-permute-start.21 = (bf16[256,512]{1,0:T(8,128)(2,1)S(1)}, bf16[256,512]{1,0:T(8,128)(2,1)S(1)}, u32[]{:S(2)}, u32[]{:S(2)}) collective-permute-start(bf16[256,512]{1,0:T(8,128)(2,1)S(1)} %get-tuple-element.22.a), channel_id=1, source_target_pairs={{0,8},{1,25},{2,10},{3,27},{4,12},{5,29},{6,14},{7,31},{8,16},{9,1... | collective-permute-start | bytes 786440 | tf_op jit(solution)/shard_map/ppermute | solution.py:37
  58.0 9.2 %collective-permute-start.17 = (bf16[256,512]{1,0:T(8,128)(2,1)S(1)}, bf16[256,512]{1,0:T(8,128)(2,1)S(1)}, u32[]{:S(2)}, u32[]{:S(2)}) collective-permute-start(bf16[256,512]{1,0:T(8,128)(2,1)S(1)} %collective-permute-done.15.b), channel_id=1, source_target_pairs={{0,32},{1,97},{2,34},{3,99},{4,36},{5,101},{6,38},{7,103},{8,40},{... | collective-permute-start | bytes 786440 | tf_op jit(solution)/shard_map/ppermute | solution.py:42
  62.8 16.2 %collective-permute-start = (bf16[384,1024]{1,0:T(8,128)(2,1)S(1)}, bf16[384,1024]{1,0:T(8,128)(2,1)S(1)}, u32[]{:S(2)}, u32[]{:S(2)}) collective-permute-start(bf16[384,1024]{1,0:T(8,128)(2,1)S(1)} %bitcast.14), channel_id=1, source_target_pairs={{0,1},{1,0},{2,3},{3,2},{4,5},{5,4},{6,7},{7,6},{8,9},{9,8},{10,11... | collective-permute-start | bytes 2359304 | tf_op jit(solution)/shard_map/ppermute | solution.py:33
  67.2 6.7 %collective-permute-start.22 = (bf16[256,512]{1,0:T(8,128)(2,1)S(1)}, bf16[256,512]{1,0:T(8,128)(2,1)S(1)}, u32[]{:S(2)}, u32[]{:S(2)}) collective-permute-start(bf16[256,512]{1,0:T(8,128)(2,1)S(1)} %get-tuple-element.22.a), channel_id=1, source_target_pairs={{0,24},{1,9},{2,26},{3,11},{4,28},{5,13},{6,30},{7,15},{8,0},{9,17... | collective-permute-start | bytes 786440 | tf_op jit(solution)/shard_map/ppermute | solution.py:38
  67.2 8.0 %collective-permute-start.23 = (bf16[256,512]{1,0:T(8,128)(2,1)S(1)}, bf16[256,512]{1,0:T(8,128)(2,1)S(1)}, u32[]{:S(2)}, u32[]{:S(2)}) collective-permute-start(bf16[256,512]{1,0:T(8,128)(2,1)S(1)} %collective-permute-done.21.b), channel_id=1, source_target_pairs={{0,8},{1,25},{2,10},{3,27},{4,12},{5,29},{6,14},{7,31},{8,16},{9,1... | collective-permute-start | bytes 786440 | tf_op jit(solution)/shard_map/ppermute | solution.py:42
  70.0 9.0 %copy-start.3 = (f32[1024]{0:T(1024)S(1)}, f32[1024]{0:T(1024)}, u32[]{:S(2)}) copy-start(f32[1024]{0:T(1024)} %param.14) | copy-start | bytes 12292
  73.9 23.8 %collective-permute-start.18 = (bf16[1024,512]{1,0:T(8,128)(2,1)S(1)}, bf16[1024,512]{1,0:T(8,128)(2,1)S(1)}, u32[]{:S(2)}, u32[]{:S(2)}) collective-permute-start(bf16[1024,512]{1,0:T(8,128)(2,1)S(1)} %shard_map.137.p0), channel_id=1, source_target_pairs={{0,8},{1,25},{2,10},{3,27},{4,12},{5,29},{6,14},{7,31},{8,16},{9,1... | collective-permute-start | bytes 3145736 | tf_op jit(solution)/shard_map/ppermute | solution.py:37
  75.3 28.0 %collective-permute-start.24 = (bf16[1024,512]{1,0:T(8,128)(2,1)S(1)}, bf16[1024,512]{1,0:T(8,128)(2,1)S(1)}, u32[]{:S(2)}, u32[]{:S(2)}) collective-permute-start(bf16[1024,512]{1,0:T(8,128)(2,1)S(1)} %shard_map.139.p0), channel_id=1, source_target_pairs={{0,32},{1,97},{2,34},{3,99},{4,36},{5,101},{6,38},{7,103},{8,40},{... | collective-permute-start | bytes 3145736 | tf_op jit(solution)/shard_map/ppermute | solution.py:37
  90.1 2.7 %copy-start.2 = (bf16[96,768]{1,0:T(8,128)(2,1)S(1)}, bf16[96,768]{1,0:T(8,128)(2,1)}, u32[]{:S(2)}) copy-start(bf16[96,768]{1,0:T(8,128)(2,1)} %a.1) | copy-start | bytes 442372
  90.2 16.4 %copy-start.4 = (f32[1024]{0:T(1024)S(1)}, f32[1024]{0:T(1024)}, u32[]{:S(2)}) copy-start(f32[1024]{0:T(1024)} %param.18) | copy-start | bytes 12292
  91.2 14.8 %collective-permute-start.10 = (bf16[384,1024]{1,0:T(8,128)(2,1)S(1)}, bf16[384,1024]{1,0:T(8,128)(2,1)S(1)}, u32[]{:S(2)}, u32[]{:S(2)}) collective-permute-start(bf16[384,1024]{1,0:T(8,128)(2,1)S(1)} %get-tuple-element.18), channel_id=1, source_target_pairs={{0,1},{1,0},{2,3},{3,2},{4,5},{5,4},{6,7},{7,6},{8,9},{9,8},{10,11... | collective-permute-start | bytes 2359304 | tf_op jit(solution)/shard_map/ppermute | solution.py:33
  92.7 39.1 %collective-permute-start.19 = (bf16[1024,512]{1,0:T(8,128)(2,1)S(1)}, bf16[1024,512]{1,0:T(8,128)(2,1)S(1)}, u32[]{:S(2)}, u32[]{:S(2)}) collective-permute-start(bf16[1024,512]{1,0:T(8,128)(2,1)S(1)} %shard_map.137.p0), channel_id=1, source_target_pairs={{0,24},{1,9},{2,26},{3,11},{4,28},{5,13},{6,30},{7,15},{8,0},{9,17... | collective-permute-start | bytes 3145736 | tf_op jit(solution)/shard_map/ppermute | solution.py:38
  92.9 4.8 %collective-permute-start.28 = (bf16[96,768]{1,0:T(8,128)(2,1)S(1)}, bf16[96,768]{1,0:T(8,128)(2,1)S(1)}, u32[]{:S(2)}, u32[]{:S(2)}) collective-permute-start(bf16[96,768]{1,0:T(8,128)(2,1)S(1)} %copy-done.2), channel_id=1, source_target_pairs={{0,32},{1,97},{2,34},{3,99},{4,36},{5,101},{6,38},{7,103},{8,40},{... | collective-permute-start | bytes 442376 | tf_op jit(solution)/shard_map/ppermute | solution.py:37
  97.7 5.6 %collective-permute-start.29 = (bf16[96,768]{1,0:T(8,128)(2,1)S(1)}, bf16[96,768]{1,0:T(8,128)(2,1)S(1)}, u32[]{:S(2)}, u32[]{:S(2)}) collective-permute-start(bf16[96,768]{1,0:T(8,128)(2,1)S(1)} %copy-done.2), channel_id=1, source_target_pairs={{0,96},{1,33},{2,98},{3,35},{4,100},{5,37},{6,102},{7,39},{8,104},... | collective-permute-start | bytes 442376 | tf_op jit(solution)/shard_map/ppermute | solution.py:38
  97.7 34.1 %collective-permute-start.20 = (bf16[1024,512]{1,0:T(8,128)(2,1)S(1)}, bf16[1024,512]{1,0:T(8,128)(2,1)S(1)}, u32[]{:S(2)}, u32[]{:S(2)}) collective-permute-start(bf16[1024,512]{1,0:T(8,128)(2,1)S(1)} %collective-permute-done.18.p1), channel_id=1, source_target_pairs={{0,8},{1,25},{2,10},{3,27},{4,12},{5,29},{6,14},{7,31},{8,16},{9,1... | collective-permute-start | bytes 3145736 | tf_op jit(solution)/shard_map/ppermute | solution.py:42
  103.3 35.7 %collective-permute-start.25 = (bf16[1024,512]{1,0:T(8,128)(2,1)S(1)}, bf16[1024,512]{1,0:T(8,128)(2,1)S(1)}, u32[]{:S(2)}, u32[]{:S(2)}) collective-permute-start(bf16[1024,512]{1,0:T(8,128)(2,1)S(1)} %shard_map.139.p0), channel_id=1, source_target_pairs={{0,96},{1,33},{2,98},{3,35},{4,100},{5,37},{6,102},{7,39},{8,104},... | collective-permute-start | bytes 3145736 | tf_op jit(solution)/shard_map/ppermute | solution.py:38
  103.4 35.7 %collective-permute-start.26 = (bf16[1024,512]{1,0:T(8,128)(2,1)S(1)}, bf16[1024,512]{1,0:T(8,128)(2,1)S(1)}, u32[]{:S(2)}, u32[]{:S(2)}) collective-permute-start(bf16[1024,512]{1,0:T(8,128)(2,1)S(1)} %collective-permute-done.24.p1), channel_id=1, source_target_pairs={{0,32},{1,97},{2,34},{3,99},{4,36},{5,101},{6,38},{7,103},{8,40},{... | collective-permute-start | bytes 3145736 | tf_op jit(solution)/shard_map/ppermute | solution.py:42
  106.0 24.4 %collective-permute-start.30 = (bf16[96,768]{1,0:T(8,128)(2,1)S(1)}, bf16[96,768]{1,0:T(8,128)(2,1)S(1)}, u32[]{:S(2)}, u32[]{:S(2)}) collective-permute-start(bf16[96,768]{1,0:T(8,128)(2,1)S(1)} %collective-permute-done.28.b), channel_id=1, source_target_pairs={{0,32},{1,97},{2,34},{3,99},{4,36},{5,101},{6,38},{7,103},{8,40},{... | collective-permute-start | bytes 442376 | tf_op jit(solution)/shard_map/ppermute | solution.py:42
  130.5 3.2 %collective-permute-start.11 = (bf16[384,1024]{1,0:T(8,128)(2,1)S(1)}, bf16[384,1024]{1,0:T(8,128)(2,1)S(1)}, u32[]{:S(2)}, u32[]{:S(2)}) collective-permute-start(bf16[384,1024]{1,0:T(8,128)(2,1)S(1)} %get-tuple-element.20.own), channel_id=1, source_target_pairs={{0,1},{1,0},{2,3},{3,2},{4,5},{5,4},{6,7},{7,6},{8,9},{9,8},{10,11... | collective-permute-start | bytes 2359304 | tf_op jit(solution)/shard_map/ppermute | solution.py:33
  131.8 17.3 %collective-permute-start.31 = (bf16[384,768]{1,0:T(8,128)(2,1)S(1)}, bf16[384,768]{1,0:T(8,128)(2,1)S(1)}, u32[]{:S(2)}, u32[]{:S(2)}) collective-permute-start(bf16[384,768]{1,0:T(8,128)(2,1)S(1)} %shard_map.142.texts), channel_id=1, source_target_pairs={{0,1},{1,0},{2,3},{3,2},{4,5},{5,4},{6,7},{7,6},{8,9},{9,8},{10,11... | collective-permute-start | bytes 1769480 | tf_op jit(solution)/shard_map/ppermute | solution.py:33
  139.0 2.7 %copy-start.5 = (f32[1024]{0:T(1024)S(1)}, f32[1024]{0:T(1024)}, u32[]{:S(2)}) copy-start(f32[1024]{0:T(1024)} %param.21) | copy-start | bytes 12292
  139.1 2.7 %copy-start.1 = (bf16[1024,768]{1,0:T(8,128)(2,1)S(1)}, bf16[1024,768]{1,0:T(8,128)(2,1)}, u32[]{:S(2)}) copy-start(bf16[1024,768]{1,0:T(8,128)(2,1)} %project.1) | copy-start | bytes 4718596
  140.5 1.3 collective-permute-start.27
  141.8 14.3 %copy-start.6 = (s32[768]{0:T(1024)S(1)}, s32[768]{0:T(1024)}, u32[]{:S(2)}) copy-start(s32[768]{0:T(1024)} %captions.1) | copy-start | bytes 9220
  143.1 24.2 %copy-start.8 = (f32[6]{0:T(128)S(1)}, f32[6]{0:T(128)}, u32[]{:S(2)}) copy-start(f32[6]{0:T(128)} %baseline.1) | copy-start | bytes 76
  143.1 13.0 %all-to-all-start = ((bf16[16,8,768]{2,1,0:T(8,128)(2,1)}), bf16[16,8,768]{2,1,0:T(8,128)(2,1)S(1)}, u32[]{:S(2)}, u32[]{:S(2)}) async-start(bf16[16,8,768]{2,1,0:T(8,128)(2,1)} %shard_map.141), calls=%async_computation | async-start | bytes 393216 | tf_op jit(solution)/shard_map/all_to_all | solution.py:320
